TPU v7x, 32 devices: a whole 2x2x4 slice. The times are simulated.
32 devices in a mesh: hot: 8 (over z, y), cold: 4 (over x, core).
Axes of the slice: x: 2, y: 2, z: 4, core: 2. Of those that a mesh axis runs over, the one named last changes fastest.
Arguments:
- tokens: bfloat16 [64, 8192], replicated, may hold values from -6 to 6
- norm_gain: float32 [8192], replicated, may hold values from 0.1 to 1.9
- hot_gate: bfloat16 [512, 8192], P(('hot', 'cold')), may hold values from -0.0625 to 0.0625
- hot_up: bfloat16 [512, 8192], P(('hot', 'cold')), may hold values from -0.0625 to 0.0625
- hot_down: bfloat16 [512, 8192], P(('hot', 'cold')), may hold values from -0.09375 to 0.09375
- hot_index: int32 [512], replicated, may hold values from 0 to 14335, as said below
- cold_gate: bfloat16 [8192, 14336], P('hot', 'cold'), may hold values from -0.0625 to 0.0625
- cold_up: bfloat16 [8192, 14336], P('hot', 'cold'), may hold values from -0.0625 to 0.0625
- cold_down: bfloat16 [14336, 8192], P('cold', 'hot'), may hold values from -0.0625 to 0.0625
- block_mask: int32 [64, 112], P(None, 'cold'), may hold values from 0 to 1, as said below
Outputs:
- ffn_out: bfloat16 [64, 8192], P(None, ('hot', 'cold'))
Inputs may be any that keep to these rules, and one draw needn't show every extreme that they name: `hot_index`: distinct hidden units. `block_mask`: in each run of 28 blocks held by one index of cold, at most 14 blocks are active for any sequence, and some index reaches exactly 14.
All inputs are finite; a program needn't handle non-finite values.
Results may differ from a plain program's by a relative error of at most 0.0065.
Values may be sent and summed in bfloat16 or wider, within the bound.
No kernel may reach another device: no remote copies, remote signals or barrier semaphores. Data moves between devices by JAX's collectives and lax.ppermute only.
A program may use at most 64 MiB of HBM per device.

v0:
```python
import jax
import jax.numpy as jnp
from jax import lax
from jax.sharding import PartitionSpec as P

UNITS = 14336


def on_device(
    tokens,
    norm_gain,
    hot_gate,
    hot_up,
    hot_down,
    hot_index,
    cold_gate,
    cold_up,
    cold_down,
    block_mask,
):
    values = tokens.astype(jnp.float32)
    scale = lax.rsqrt(jnp.mean(values * values, axis=1, keepdims=True) + 1e-05)
    normed = (values * scale * norm_gain[None, :]).astype(jnp.bfloat16)
    dims = (((1,), (1,)), ((), ()))
    gate_hot = lax.dot_general(normed, hot_gate, dims, preferred_element_type=jnp.float32)
    up_hot = lax.dot_general(normed, hot_up, dims, preferred_element_type=jnp.float32)
    hidden_hot = (jax.nn.silu(gate_hot) * up_hot).astype(jnp.bfloat16)
    feat_rows = cold_gate.shape[0]
    unit_count = cold_gate.shape[1]
    blocks_here = block_mask.shape[1]
    block = unit_count // blocks_here
    seqs = tokens.shape[0]
    is_hot = jnp.zeros((UNITS,), jnp.float32).at[hot_index].set(1.0)
    local_hot = lax.dynamic_slice_in_dim(is_hot, lax.axis_index("cold") * unit_count, unit_count)
    normed_part = lax.dynamic_slice_in_dim(normed, lax.axis_index("hot") * feat_rows, feat_rows, 1)
    gate_w, up_w, down_w = (cold_gate, cold_up, cold_down)
    seq_live = block_mask.astype(jnp.float32)
    unit_live = (1.0 - local_hot).reshape(blocks_here, block)
    live = (seq_live[:, :, None] * unit_live[None, :, :]).reshape(seqs, unit_count)
    gate_part = jnp.dot(normed_part, gate_w, preferred_element_type=jnp.float32)
    up_part = jnp.dot(normed_part, up_w, preferred_element_type=jnp.float32)
    gate_cold, up_cold = lax.psum((gate_part, up_part), "hot")
    hidden_cold = (jax.nn.silu(gate_cold) * up_cold * live).astype(jnp.bfloat16)
    out_cold = jnp.dot(hidden_cold, down_w, preferred_element_type=jnp.float32)
    down_cols = lax.all_to_all(hot_down, ("hot", "cold"), split_axis=1, concat_axis=0, tiled=True)
    hidden_all = lax.all_gather(hidden_hot, ("hot", "cold"), axis=1, tiled=True)
    hot_total = jnp.dot(hidden_all, down_cols, preferred_element_type=jnp.float32)
    cold_total = lax.psum_scatter(out_cold, "cold", scatter_dimension=1, tiled=True)
    total = hot_total + cold_total
    return total.astype(jnp.bfloat16)


def solution(mesh):
    in_specs = (
        P(),
        P(),
        P(("hot", "cold"), None),
        P(("hot", "cold"), None),
        P(("hot", "cold"), None),
        P(),
        P("hot", "cold"),
        P("hot", "cold"),
        P("cold", "hot"),
        P(None, "cold"),
    )
    out_specs = P(None, ("hot", "cold"))
    return jax.shard_map(
        on_device, mesh=mesh, in_specs=in_specs, out_specs=out_specs, check_vma=False
    )
```

profile of v0, /device:TPU:0, one launch (start us, length us, event | category | flops | bytes accessed | tf_op | source)
XLA Modules:
  0.0 177.9 jit_solution(3256755410243305480)
XLA Ops:
  6.5 1.6 fusion
  8.1 0.0 slice-start
  8.1 1.7 fusion.2
  9.8 0.0 slice-start.1
  9.8 5.6 %fusion.11 = f32[64,3584]{1,0:T(8,128)} fusion(bf16[1024,3584]{1,0:T(8,128)(2,1)} %param.17, bf16[64,8192]{1,0:T(8,128)(2,1)S(1)} %fusion.2, s32[]{:T(128)S(6)} %select_n.9), kind=kOutput, calls=%fused_computation.17 | convolution fusion | flops 469762048 | bytes 8388612 | tf_op jit(solution)/shard_map/dot_general | solution.py:41
  15.4 0.0 copy-start.3
  15.5 0.0 copy-start.4
  15.5 2.3 %fusion.13 = f32[64,3584]{1,0:T(8,128)} fusion(bf16[1024,3584]{1,0:T(8,128)(2,1)S(1)} %bitcast.25, bf16[64,8192]{1,0:T(8,128)(2,1)S(1)} %fusion.2, s32[]{:T(128)S(6)} %select_n.9), kind=kOutput, calls=%fused_computation.19 | convolution fusion | flops 469762048 | bytes 8388612 | tf_op jit(solution)/shard_map/dot_general | solution.py:40
  17.8 0.0 all-reduce.3.cloned.1.call-update
  17.8 0.0 copy-start.1
  17.8 0.7 copy.22
  18.5 7.3 %all-to-all-start = ((bf16[16,32,256]{2,0,1:T(8,128)(2,1)}), bf16[16,32,256]{2,0,1:T(8,128)(2,1)S(1)}, u32[]{:S(2)}, u32[]{:S(2)}) async-start(bf16[16,32,256]{2,0,1:T(8,128)(2,1)} %bitcast.23), calls=%async_computation | async-start | bytes 524288 | tf_op jit(solution)/shard_map/all_to_all | solution.py:45
  25.9 0.0 reduce-scatter.2.cloned.1.call-start
  26.0 0.1 copy.16
  26.1 2.5 %scatter_custom_fusion = f32[14336]{0:T(1024)S(1)} fusion(s32[512]{0:T(512)S(1)} %compare_select_fusion, f32[512]{0:T(512)S(1)} %broadcast.20, f32[]{:T(128)} %constant.12.clone.1), kind=kCustom, calls=%fused_computation.21 | custom fusion | bytes 57348 | tf_op jit(solution)/shard_map/scatter | solution.py:33
  28.6 0.1 dynamic-slice_subtract_fusion
  28.6 93.3 %all-reduce.3.cloned.1.call-done = (f32[64,3584]{1,0:T(8,128)}, f32[64,3584]{1,0:T(8,128)}) async-done(((f32[64,3584]{1,0:T(8,128)}, f32[64,3584]{1,0:T(8,128)}), (f32[64,3584]{1,0:T(8,128)}, f32[64,3584]{1,0:T(8,128)})) %all-reduce.3.cloned.1.call-update) | async-done | bytes 1835024 | tf_op jit(solution)/shard_map/psum | solution.py:42
  121.9 0.3 mul.68
  122.3 6.2 %fusion.7 = f32[64,1024]{1,0:T(8,128)} fusion(bf16[3584,1024]{1,0:T(8,128)(2,1)} %param.18, f32[8,8,28,128]{3,2,1,0:T(8,128)S(1)} %bitcast.26, f32[64,3584]{1,0:T(8,128)} %get-tuple-element.5, f32[64,3584]{1,0:T(8,128)} %get-tuple-element.6, f32[3584]{0:T(1024)S(1)} %dynamic-slice_subtract_fusion), kind=kOutput, calls=%fused_computation.13 | convolution fusion | flops 471597056 | bytes 10369024 | tf_op jit(solution)/shard_map/dot_general | solution.py:44
  128.5 0.0 reduce-scatter.2.cloned.1.call-update
  128.5 0.4 fusion.20
  128.9 0.4 fusion.4
  129.3 40.1 %all_gather.3 = bf16[64,512]{0,1:T(8,128)(2,1)S(1)} all-gather(bf16[64,16]{0,1:T(8,128)(2,1)S(1)} %fusion.4), channel_id=1, replica_groups=mesh['hot'=8,'cold'=4] {'hot','cold'}, dimensions={1}, use_global_device_ids=true | all-gather | bytes 67584 | tf_op jit(solution)/shard_map/all_gather | solution.py:46
  169.4 1.7 fusion.3
  (17 shorter events, 0.0 us)
Async XLA Ops:
  6.5 122.0 %copy-start = (bf16[16,8192]{1,0:T(8,128)(2,1)S(1)}, bf16[16,8192]{1,0:T(8,128)(2,1)}, u32[]{:S(2)}) copy-start(bf16[16,8192]{1,0:T(8,128)(2,1)} %param.12) | copy-start | bytes 786436
  6.5 115.4 %all-reduce.3.cloned.1.call-start = ((), (), s32[]{:S(2)}) async-start(), calls=%async_computation.3 | async-start | bytes 3670016 | tf_op jit(solution)/shard_map/psum | solution.py:42
  8.1 7.3 %slice-start = ((s8[7340032]{0:T(1024)(128)(4,1)}), s8[4194304]{0:T(1024)(128)(4,1)S(1)}, s32[]{:S(2)}) async-start(s8[7340032]{0:T(1024)(128)(4,1)} %bitcast.24), calls=%async_computation.4 | async-start | bytes 8388608
  9.8 5.6 %slice-start.1 = ((s8[7340032]{0:T(1024)(128)(4,1)}), s8[3145728]{0:T(1024)(128)(4,1)S(1)}, s32[]{:S(2)}) async-start(s8[7340032]{0:T(1024)(128)(4,1)} %bitcast.24), calls=%async_computation.5 | async-start | bytes 6291456
  15.4 2.4 %copy-start.2 = (bf16[16,8192]{1,0:T(8,128)(2,1)S(1)}, bf16[16,8192]{1,0:T(8,128)(2,1)}, u32[]{:S(2)}) copy-start(bf16[16,8192]{1,0:T(8,128)(2,1)} %param.14) | copy-start | bytes 786436
  15.4 10.5 %copy-start.3 = (s32[64,28]{0,1:T(8,128)S(1)}, s32[64,28]{0,1:T(8,128)}, u32[]{:S(2)}) copy-start(s32[64,28]{0,1:T(8,128)} %param.19) | copy-start | bytes 21508
  15.5 10.6 %copy-start.4 = (s32[512]{0:T(512)S(1)}, s32[512]{0:T(512)}, u32[]{:S(2)}) copy-start(s32[512]{0:T(512)} %param.15) | copy-start | bytes 6148
  17.8 111.1 %copy-start.1 = (bf16[16,8192]{1,0:T(8,128)(2,1)S(1)}, bf16[16,8192]{1,0:T(8,128)(2,1)}, u32[]{:S(2)}) copy-start(bf16[16,8192]{1,0:T(8,128)(2,1)} %param.13) | copy-start | bytes 786436
  18.5 150.8 %all-to-all-start = ((bf16[16,32,256]{2,0,1:T(8,128)(2,1)}), bf16[16,32,256]{2,0,1:T(8,128)(2,1)S(1)}, u32[]{:S(2)}, u32[]{:S(2)}) async-start(bf16[16,32,256]{2,0,1:T(8,128)(2,1)} %bitcast.23), calls=%async_computation | async-start | bytes 524288 | tf_op jit(solution)/shard_map/all_to_all | solution.py:45
  25.9 143.5 %reduce-scatter.2.cloned.1.call-start = ((), (), s32[]{:S(2)}) async-start(), calls=%async_computation.2 | async-start | bytes 327680 | tf_op jit(solution)/shard_map/reduce_scatter | solution.py:48
Sparse Core Ops, SparseCore 0:
  17.9 103.9 all-reduce.2
  128.6 19.6 reduce-scatter.1
where the time goes:
time: 178 us
  waiting for transfers between devices  93.3 us (52%)
  blocking collectives  40.1 us (23%)
  matrix products  16.5 us (9%)
  between operations  13.5 us (8%)
  starting transfers between devices  7.37 us (4%)
  local copies, waits for them, and re-layouts  3.65 us (2%)
  other arithmetic  3.35 us (2%)
    psum x1, waiting for transfers between devices, on_device(): gate_cold, up_cold = lax.psum((gate_part, up_part), 'hot')  93.3 us
    all_gather x1, blocking collectives, on_device(): hidden_all = lax.all_gather(hidden_hot, ('hot', 'cold'), axis=1, tiled=True)  40.1 us
    all_to_all x1, starting transfers between devices, on_device(): lax.all_to_all(hot_down, ('hot', 'cold'), split_axis=1, concat_axis=0, ti...  7.32 us
    dot_general x1, matrix products, on_device(): out_cold = jnp.dot(hidden_cold, down_w, preferred_element_type=jnp.float32)  6.19 us
    dot_general x1, matrix products, on_device(): up_part = jnp.dot(normed_part, up_w, preferred_element_type=jnp.float32)  5.59 us
  transfers between devices with their start and end apart: 3, of which 1 were waited for; matrix products, arithmetic and copies ran while one was open for 6% of the time, Pallas kernels for 0%

commit v1 on v0

v1 whole, which is shorter than its diff:
```python
import functools

import jax
import jax.numpy as jnp
from jax import lax
from jax.experimental import pallas as pl
from jax.experimental.pallas import tpu as pltpu
from jax.sharding import PartitionSpec as P

F32 = jnp.float32
BF16 = jnp.bfloat16
ANY = pl.BlockSpec(memory_space=pl.ANY)
VMEM = pl.BlockSpec(memory_space=pltpu.VMEM)
SMEM = pl.BlockSpec(memory_space=pltpu.SMEM)
NT = (((1,), (1,)), ((), ()))


def silu(v):
    return v / (1.0 + jnp.exp(-v))


def partial_kernel(
    tokens, gain, hot_gate, hot_up, hot_index, cold_gate, cold_up, mask,
    out, live, picks,
    tok_v, gain_v, hot_v, hidx_v, mask_v, normed_v, unit_v, w_v, in_sem, w_sem,
    *, slots, block, n_hot,
):
    seqs, width = tok_v.shape
    feats = cold_gate.shape[0]
    blocks = mask.shape[1]
    rows = hot_gate.shape[0]
    h = lax.axis_index("hot")
    c = lax.axis_index("cold")
    loads = [
        pltpu.make_async_copy(mask, mask_v, in_sem.at[0]),
        pltpu.make_async_copy(tokens, tok_v, in_sem.at[1]),
        pltpu.make_async_copy(gain, gain_v, in_sem.at[2]),
        pltpu.make_async_copy(hot_index, hidx_v, in_sem.at[3]),
        pltpu.make_async_copy(hot_gate, hot_v.at[pl.ds(0, rows)], in_sem.at[4]),
        pltpu.make_async_copy(hot_up, hot_v.at[pl.ds(rows, rows)], in_sem.at[5]),
    ]
    for load in loads:
        load.start()
    loads[0].wait()
    alive = jnp.max(mask_v[...].astype(F32), axis=0, keepdims=True)
    tri = (
        lax.broadcasted_iota(jnp.int32, (blocks, blocks), 0)
        <= lax.broadcasted_iota(jnp.int32, (blocks, blocks), 1)
    ).astype(F32)
    rank = jnp.dot(jnp.broadcast_to(alive, (8, blocks)), tri, preferred_element_type=F32)[:1]
    rank = jnp.where(alive > 0.0, rank, 0.0)
    lane = lax.broadcasted_iota(jnp.int32, (1, blocks), 1)
    lane_f = lane.astype(F32)
    count = jnp.sum(alive).astype(jnp.int32)
    picks[slots] = count
    index = []
    for j in range(slots):
        index.append(jnp.sum(jnp.where(rank == float(j + 1), lane_f, 0.0)).astype(jnp.int32))

    def copies(j):
        cols = pl.ds(pl.multiple_of(index[j] * block, block), block)
        return (
            pltpu.make_async_copy(
                cold_gate.at[:, cols], w_v.at[j, :, pl.ds(0, block)], w_sem.at[0, j]
            ),
            pltpu.make_async_copy(
                cold_up.at[:, cols], w_v.at[j, :, pl.ds(block, block)], w_sem.at[1, j]
            ),
        )

    for j in range(slots):
        picks[j] = index[j]

        @pl.when(j < count)
        def _():
            for copy in copies(j):
                copy.start()

    loads[1].wait()
    loads[2].wait()
    values = tok_v[...].astype(F32)
    scale = lax.rsqrt(jnp.mean(values * values, axis=1, keepdims=True) + 1e-05)
    normed_v[...] = (values * scale * gain_v[...]).astype(BF16)

    loads[3].wait()
    hidx = hidx_v[...] - c * (blocks * block)
    owner = lax.shift_right_arithmetic(hidx, jnp.int32(block.bit_length() - 1))
    inner = jnp.bitwise_and(hidx, jnp.int32(block - 1))
    n = hidx.shape[1]
    by_block = (lax.broadcasted_iota(jnp.int32, (blocks, n), 0) == owner).astype(F32)
    by_unit = (lax.broadcasted_iota(jnp.int32, (block, n), 0) == inner).astype(F32)
    unit_v[...] = 1.0 - lax.dot_general(by_block, by_unit, NT, preferred_element_type=F32)
    chunk = live.shape[0]
    seq_mask = mask_v[pl.ds(h * chunk, chunk), :].astype(F32)
    for j in range(slots):
        seq_live = jnp.sum(
            jnp.where(lane == index[j], seq_mask, 0.0), axis=1, keepdims=True
        ) * jnp.where(j < count, 1.0, 0.0)
        live[:, pl.ds(j * block, block)] = seq_live * unit_v[pl.ds(index[j], 1), :]

    loads[4].wait()
    loads[5].wait()
    both = lax.dot_general(normed_v[...], hot_v[...], NT, preferred_element_type=F32)
    hidden_hot = (silu(both[:, :rows]) * both[:, rows:]).astype(BF16)
    spread = (
        lax.broadcasted_iota(jnp.int32, (rows, rows * n_hot), 1)
        == lax.broadcasted_iota(jnp.int32, (rows, rows * n_hot), 0) + h * rows
    ).astype(BF16)
    out[:, pl.ds(2 * slots * block, rows * n_hot)] = jnp.dot(
        hidden_hot, spread, preferred_element_type=F32
    ).astype(BF16)

    part = normed_v[:, pl.ds(pl.multiple_of(h * feats, feats), feats)]
    for j in range(slots):
        cols = pl.ds(2 * j * block, 2 * block)

        @pl.when(j < count)
        def _():
            for copy in copies(j):
                copy.wait()
            out[:, cols] = jnp.dot(part, w_v[j], preferred_element_type=F32).astype(BF16)

        @pl.when(j >= count)
        def _():
            out[:, cols] = jnp.zeros((seqs, 2 * block), BF16)


def hidden_kernel(parts, live, out, *, slots, block, n_hot):
    chunk = live.shape[0]
    total = parts[pl.ds(0, chunk), :].astype(F32)
    for src in range(1, n_hot):
        total = total + parts[pl.ds(src * chunk, chunk), :].astype(F32)
    pieces = []
    for j in range(slots):
        gate = total[:, 2 * j * block : (2 * j + 1) * block]
        up = total[:, (2 * j + 1) * block : (2 * j + 2) * block]
        pieces.append((silu(gate) * up * live[:, pl.ds(j * block, block)]).astype(BF16))
    pieces.append(total[:, 2 * slots * block :].astype(BF16))
    hidden = jnp.concatenate(pieces, axis=1)
    for dst in range(n_hot):
        out[pl.ds(dst * chunk, chunk), :] = hidden


def down_kernel(picks, hidden, hot_rows, cold_down, out, w_v, sem, hot_sem, *, slots, block):
    count = picks[slots]
    base = slots * block

    def copy(j):
        rows = pl.ds(pl.multiple_of(picks[j] * block, block), block)
        return pltpu.make_async_copy(
            cold_down.at[rows], w_v.at[pl.ds(j * block, block)], sem.at[j]
        )

    hot_copy = pltpu.make_async_copy(hot_rows, w_v.at[pl.ds(base, hot_rows.shape[0])], hot_sem.at[0])
    for j in range(slots):

        @pl.when(j < count)
        def _():
            copy(j).start()

        @pl.when(j >= count)
        def _():
            w_v[pl.ds(j * block, block), :] = jnp.zeros((block, w_v.shape[1]), BF16)

    hot_copy.start()
    for j in range(slots):

        @pl.when(j < count)
        def _():
            copy(j).wait()

    hot_copy.wait()
    total = jnp.dot(hidden[...], w_v[...], preferred_element_type=F32)
    n_cold, _, cols = out.shape
    for k in range(n_cold):
        out[k] = total[:, k * cols : (k + 1) * cols].astype(out.dtype)


def on_device(
    tokens, norm_gain, hot_gate, hot_up, hot_down, hot_index,
    cold_gate, cold_up, cold_down, block_mask, *, n_hot, n_cold,
):
    seqs, width = tokens.shape
    feats, units = cold_gate.shape
    blocks = block_mask.shape[1]
    block = units // blocks
    slots = blocks // 2
    rows = hot_gate.shape[0]
    hots = hot_index.shape[0]
    chunk = seqs // n_hot
    hot_lanes = rows * n_hot
    cols = cold_down.shape[1]

    down_rows = lax.all_to_all(hot_down, "hot", split_axis=1, concat_axis=0, tiled=True)

    parts, live, picks = pl.pallas_call(
        functools.partial(partial_kernel, slots=slots, block=block, n_hot=n_hot),
        name="partial",
        in_specs=[ANY] * 8,
        out_specs=[VMEM, VMEM, SMEM],
        out_shape=[
            jax.ShapeDtypeStruct((seqs, 2 * slots * block + hot_lanes), BF16),
            jax.ShapeDtypeStruct((chunk, slots * block), F32),
            jax.ShapeDtypeStruct((slots + 1,), jnp.int32),
        ],
        scratch_shapes=[
            pltpu.VMEM((seqs, width), BF16),
            pltpu.VMEM((1, width), F32),
            pltpu.VMEM((2 * rows, width), BF16),
            pltpu.VMEM((1, hots), jnp.int32),
            pltpu.VMEM((seqs, blocks), jnp.int32),
            pltpu.VMEM((seqs, width), BF16),
            pltpu.VMEM((blocks, block), F32),
            pltpu.VMEM((slots, feats, 2 * block), BF16),
            pltpu.SemaphoreType.DMA((6,)),
            pltpu.SemaphoreType.DMA((2, slots)),
        ],
    )(
        tokens, norm_gain[None, :], hot_gate, hot_up, hot_index[None, :],
        cold_gate, cold_up, block_mask,
    )
    parts = lax.all_to_all(parts, "hot", split_axis=0, concat_axis=0, tiled=True)
    hidden = pl.pallas_call(
        functools.partial(hidden_kernel, slots=slots, block=block, n_hot=n_hot),
        name="hidden",
        in_specs=[VMEM, VMEM],
        out_specs=VMEM,
        out_shape=jax.ShapeDtypeStruct((seqs, slots * block + hot_lanes), BF16),
    )(parts, live)
    hidden = lax.all_to_all(hidden, "hot", split_axis=0, concat_axis=0, tiled=True)
    out = pl.pallas_call(
        functools.partial(down_kernel, slots=slots, block=block),
        name="down",
        in_specs=[SMEM, VMEM, ANY, ANY],
        out_specs=VMEM,
        out_shape=jax.ShapeDtypeStruct((n_cold, seqs, cols // n_cold), BF16),
        scratch_shapes=[
            pltpu.VMEM((slots * block + hot_lanes, cols), BF16),
            pltpu.SemaphoreType.DMA((slots,)),
            pltpu.SemaphoreType.DMA((1,)),
        ],
    )(picks, hidden, down_rows, cold_down)
    out = lax.all_to_all(out, "cold", split_axis=0, concat_axis=0, tiled=True)
    return jnp.sum(out.astype(F32), axis=0).astype(BF16)


def solution(mesh):
    in_specs = (
        P(),
        P(),
        P(("hot", "cold"), None),
        P(("hot", "cold"), None),
        P(("hot", "cold"), None),
        P(),
        P("hot", "cold"),
        P("hot", "cold"),
        P("cold", "hot"),
        P(None, "cold"),
    )
    body = functools.partial(on_device, n_hot=mesh.shape["hot"], n_cold=mesh.shape["cold"])
    return jax.shard_map(
        body, mesh=mesh, in_specs=in_specs, out_specs=P(None, ("hot", "cold")), check_vma=False
    )
```

time: 178 us -> 65.5 us (0.37)
  waiting for transfers between devices: 93.3 us -> 20.9 us
  blocking collectives: 40.1 us -> 20 us
  matrix products: 16.5 us -> 0 us
  between operations: 13.5 us -> 0.03 us
  Pallas kernels: 0 us -> 10.5 us
  starting transfers between devices: 7.37 us -> 11.5 us
  other arithmetic: 3.35 us -> 0.64 us
    psum x1 -> x0, waiting for transfers between devices: 93.3 us -> none  [on_device(): gate_cold, up_cold = lax.psum((gate_part, up_part), 'hot')]
    all_gather x1 -> x0, blocking collectives: 40.1 us -> none  [on_device(): hidden_all = lax.all_gather(hidden_hot, ('hot', 'cold'), axis=1, tiled=True)]
    all_to_all x1 -> x2, waiting for transfers between devices: 0.01 us -> 20.9 us  [the longest x1 13.5 us: on_device(): lax.all_to_all(parts, 'hot', split_axis=0, concat_axis=0, tiled=True)]
    all_to_all x0 -> x2, blocking collectives: none -> 20 us  [the longest x1 12.1 us: on_device(): lax.all_to_all(hidden, 'hot', split_axis=0, concat_axis=0, tiled=True)]
    dot_general x6 -> x0, matrix products: 16.5 us -> none  [the longest x1 6.19 us: on_device(): out_cold = jnp.dot(hidden_cold, down_w, preferred_element_type=jnp.float32)]
    pallas_call x0 -> x3, Pallas kernels: none -> 10.5 us  [the longest x1 4.83 us: on_device(): pl.pallas_call(functools.partial(partial_kernel, slots=slots, block=block...]
    all_to_all x1 -> x2, starting transfers between devices: 7.32 us -> 11.5 us  [the longest x1 7.32 us: on_device(): lax.all_to_all(parts, 'hot', split_axis=0, concat_axis=0, tiled=True)]
    scatter x1 -> x0, local copies, waits for them, and re-layouts: 2.48 us -> none  [on_device(): is_hot = jnp.zeros((UNITS,), jnp.float32).at[hot_index].set(1.0)]
  transfers between devices with their start and end apart: 3 -> 2, of which waited for: 1 -> 2; matrix products, arithmetic and copies ran while one was open for 6% -> 1% of each run, Pallas kernels for 0% -> 3%
where the time goes in v1:
time: 65.5 us; the launch traced here: 65.8 us
  waiting for transfers between devices  20.9 us (32%)
  blocking collectives  20 us (31%)
  starting transfers between devices  11.5 us (18%)
  Pallas kernels  10.5 us (16%)
  local copies, waits for them, and re-layouts  2.14 us (3%)
    all_to_all x1, waiting for transfers between devices, on_device(): lax.all_to_all(parts, 'hot', split_axis=0, concat_axis=0, tiled=True)  13.5 us
    all_to_all x1, blocking collectives, on_device(): lax.all_to_all(hidden, 'hot', split_axis=0, concat_axis=0, tiled=True)  12.1 us
    all_to_all x1, blocking collectives, on_device(): out = lax.all_to_all(out, 'cold', split_axis=0, concat_axis=0, tiled=True)  7.9 us
    all_to_all x1, waiting for transfers between devices, on_device(): lax.all_to_all(hot_down, 'hot', split_axis=1, concat_axis=0, tiled=True)  7.38 us
    all_to_all x1, starting transfers between devices, on_device(): lax.all_to_all(parts, 'hot', split_axis=0, concat_axis=0, tiled=True)  7.32 us
    pallas_call x1, Pallas kernels, on_device(): pl.pallas_call(functools.partial(partial_kernel, slots=slots, block=block...  4.83 us
    all_to_all x1, starting transfers between devices, on_device(): lax.all_to_all(hot_down, 'hot', split_axis=1, concat_axis=0, tiled=True)  4.21 us
    pallas_call x1, Pallas kernels, on_device(): pl.pallas_call(functools.partial(down_kernel, slots=slots, block=block),...  3.87 us
  transfers between devices with their start and end apart: 2, of which 2 were waited for; matrix products, arithmetic and copies ran while one was open for 1% of the time, Pallas kernels for 3%

profile of v1, /device:TPU:0, one launch (start us, length us, event | category | flops | bytes accessed | tf_op | source)
XLA Modules:
  0.0 65.8 jit_solution(271140156584921520)
XLA Ops:
  0.0 1.4 %copy.11.mask = s32[64,28]{1,0:T(8,128)} copy(s32[64,28]{0,1:T(8,128)} %param.19) | data formatting | bytes 14336 | tf_op args[9]
  1.4 0.0 copy-start.2
  1.4 4.8 %partial.1 = (bf16[64,3712]{1,0:T(8,128)(2,1)}, f32[8,1792]{1,0:T(8,128)}, s32[15]{0:T(128)}) custom-call(bf16[64,8192]{1,0:T(8,128)(2,1)} %tokens.1, f32[1,8192]{1,0:T(1,128)} %bitcast.19, bf16[16,8192]{1,0:T(8,128)(2,1)} %hot_gate.1, bf16[16,8192]{1,0:T(8,128)(2,1)} %hot_up.1, s32[1,512]{1,0:T(1,128)} %bitcast.20, bf16[1024,3584]{1,0:T(8,128)(2,1)} %cold_gate.1, ...), custom_call_target="tpu_custom_call" | custom-call | tf_op jit(solution)/shard_map/partial/pallas_call | solution.py:196
  6.3 7.3 %all-to-all-start = ((bf16[8,8,3712]{2,1,0:T(8,128)(2,1)}), bf16[8,8,3712]{2,1,0:T(8,128)(2,1)S(1)}, u32[]{:S(2)}, u32[]{:S(2)}) async-start(bf16[8,8,3712]{2,1,0:T(8,128)(2,1)} %bitcast.17), calls=%async_computation | async-start | bytes 950272 | tf_op jit(solution)/shard_map/all_to_all | solution.py:222
  13.6 0.0 copy-done.2
  13.6 0.7 %copy.15 = bf16[2,8,8,1024]{3,2,0,1:T(8,128)(2,1)} copy(bf16[2,8,8,1024]{3,2,1,0:T(8,128)(2,1)S(1)} %bitcast.18) | data formatting | bytes 524288 | tf_op jit(solution)/shard_map/all_to_all | solution.py:194
  14.3 13.5 %all-to-all-done = bf16[8,8,3712]{2,1,0:T(8,128)(2,1)S(1)} async-done(((bf16[8,8,3712]{2,1,0:T(8,128)(2,1)}), bf16[8,8,3712]{2,1,0:T(8,128)(2,1)S(1)}, u32[]{:S(2)}, u32[]{:S(2)}) %all-to-all-start) | async-done | bytes 475168 | tf_op jit(solution)/shard_map/all_to_all | solution.py:222
  27.8 0.0 copy-start
  27.8 4.2 %all-to-all-start.2 = ((bf16[16,8,1024]{2,0,1:T(8,128)(2,1)}), bf16[16,8,1024]{2,0,1:T(8,128)(2,1)S(1)}, u32[]{:S(2)}, u32[]{:S(2)}) async-start(bf16[16,8,1024]{2,0,1:T(8,128)(2,1)} %bitcast.12), calls=%async_computation.2 | async-start | bytes 524288 | tf_op jit(solution)/shard_map/all_to_all | solution.py:194
  32.0 0.0 copy-done
  32.0 1.8 %hidden.1 = bf16[64,1920]{1,0:T(8,128)(2,1)} custom-call(bf16[64,3712]{1,0:T(8,128)(2,1)} %bitcast.13, f32[8,1792]{1,0:T(8,128)} %get-tuple-element.10.live), custom_call_target="tpu_custom_call" | custom-call | tf_op jit(solution)/shard_map/hidden/pallas_call | solution.py:223
  33.8 7.4 %all-to-all-done.2 = bf16[16,8,1024]{2,0,1:T(8,128)(2,1)S(1)} async-done(((bf16[16,8,1024]{2,0,1:T(8,128)(2,1)}), bf16[16,8,1024]{2,0,1:T(8,128)(2,1)S(1)}, u32[]{:S(2)}, u32[]{:S(2)}) %all-to-all-start.2) | async-done | bytes 262176 | tf_op jit(solution)/shard_map/all_to_all | solution.py:194
  41.2 0.0 copy-start.1
  41.2 12.1 %all_to_all.46 = bf16[8,8,1920]{2,1,0:T(8,128)(2,1)} all-to-all(bf16[8,8,1920]{2,1,0:T(8,128)(2,1)} %bitcast.15), channel_id=1, replica_groups=mesh['hot'=8,'cold'=4] {'hot'}, dimensions={0} | all-to-all | bytes 491520 | tf_op jit(solution)/shard_map/all_to_all | solution.py:230
  53.4 0.0 copy-done.1
  53.4 3.9 %down.1 = bf16[4,64,256]{2,1,0:T(8,128)(2,1)} custom-call(s32[15]{0:T(128)} %get-tuple-element.8.picks, bf16[64,1920]{1,0:T(8,128)(2,1)} %bitcast.16, bf16[128,1024]{1,0:T(8,128)(2,1)} %bitcast.14, bf16[3584,1024]{1,0:T(8,128)(2,1)} %cold_down.1), custom_call_target="tpu_custom_call" | custom-call | tf_op jit(solution)/shard_map/down/pallas_call | solution.py:231
  57.2 7.9 %all_to_all.47 = bf16[4,64,256]{2,1,0:T(8,128)(2,1)S(1)} all-to-all(bf16[4,64,256]{2,1,0:T(8,128)(2,1)} %down.1), channel_id=1, replica_groups=mesh['hot'=8,'cold'=4] {'cold'}, dimensions={0} | all-to-all | bytes 262144 | tf_op jit(solution)/shard_map/all_to_all | solution.py:243
  65.1 0.6 reduce_sum.12
Async XLA Ops:
  1.4 12.2 %copy-start.2 = (bf16[16,8192]{1,0:T(8,128)(2,1)S(1)}, bf16[16,8192]{1,0:T(8,128)(2,1)}, u32[]{:S(2)}) copy-start(bf16[16,8192]{1,0:T(8,128)(2,1)} %param.14) | copy-start | bytes 786436
  6.3 21.5 %all-to-all-start = ((bf16[8,8,3712]{2,1,0:T(8,128)(2,1)}), bf16[8,8,3712]{2,1,0:T(8,128)(2,1)S(1)}, u32[]{:S(2)}, u32[]{:S(2)}) async-start(bf16[8,8,3712]{2,1,0:T(8,128)(2,1)} %bitcast.17), calls=%async_computation | async-start | bytes 950272 | tf_op jit(solution)/shard_map/all_to_all | solution.py:222
  27.8 4.2 %copy-start = (bf16[8,8,3712]{2,1,0:T(8,128)(2,1)}, bf16[8,8,3712]{2,1,0:T(8,128)(2,1)S(1)}, u32[]{:S(2)}) copy-start(bf16[8,8,3712]{2,1,0:T(8,128)(2,1)S(1)} %all-to-all-done) | copy-start | bytes 1425412
  27.8 13.4 %all-to-all-start.2 = ((bf16[16,8,1024]{2,0,1:T(8,128)(2,1)}), bf16[16,8,1024]{2,0,1:T(8,128)(2,1)S(1)}, u32[]{:S(2)}, u32[]{:S(2)}) async-start(bf16[16,8,1024]{2,0,1:T(8,128)(2,1)} %bitcast.12), calls=%async_computation.2 | async-start | bytes 524288 | tf_op jit(solution)/shard_map/all_to_all | solution.py:194
  41.2 12.1 %copy-start.1 = (bf16[16,8,1024]{2,0,1:T(8,128)(2,1)}, bf16[16,8,1024]{2,0,1:T(8,128)(2,1)S(1)}, u32[]{:S(2)}) copy-start(bf16[16,8,1024]{2,0,1:T(8,128)(2,1)S(1)} %all-to-all-done.2) | copy-start | bytes 786436

commit v2 on v1

v2 whole, which is shorter than its diff:
```python
import functools

import jax
import jax.numpy as jnp
from jax import lax
from jax.experimental import pallas as pl
from jax.experimental.pallas import tpu as pltpu
from jax.sharding import PartitionSpec as P


F32 = jnp.float32
BF16 = jnp.bfloat16
ANY = pl.BlockSpec(memory_space=pl.ANY)
VMEM = pl.BlockSpec(memory_space=pltpu.VMEM)
SMEM = pl.BlockSpec(memory_space=pltpu.SMEM)
NT = (((1,), (1,)), ((), ()))


def limit(mib):
    return pltpu.CompilerParams(vmem_limit_bytes=mib << 20)


def silu(v):
    return v / (1.0 + jnp.exp(-v))


def partial_kernel(
    tokens_hbm, gain_hbm, hot_gate_hbm, hot_up_hbm, hot_index_hbm, mask_hbm, cold_gate, cold_up,
    out, live, picks,
    tokens, gain, hot_gate, hot_up, hot_index, mask, normed_v, unit_v, w_v, in_sem, w_sem,
    *, slots, block, n_hot,
):
    loads = [
        pltpu.make_async_copy(source, target, in_sem.at[i])
        for i, (source, target) in enumerate((
            (mask_hbm, mask), (tokens_hbm, tokens), (gain_hbm, gain),
            (hot_index_hbm, hot_index), (hot_gate_hbm, hot_gate), (hot_up_hbm, hot_up),
        ))
    ]
    for load in loads:
        load.start()
    loads[0].wait()
    seqs = tokens.shape[0]
    feats = cold_gate.shape[0]
    blocks = mask.shape[0]
    rows = hot_gate.shape[0]
    h = lax.axis_index("hot")
    c = lax.axis_index("cold")
    mask_f = mask[...].astype(F32)
    alive = jnp.max(mask_f, axis=1, keepdims=True)
    tri = (
        lax.broadcasted_iota(jnp.int32, (blocks, blocks), 1)
        <= lax.broadcasted_iota(jnp.int32, (blocks, blocks), 0)
    ).astype(F32)
    rank = jnp.dot(tri, jnp.broadcast_to(alive, (blocks, block)), preferred_element_type=F32)
    rank = jnp.where(alive > 0.0, rank[:, :1], 0.0)
    number = lax.broadcasted_iota(jnp.int32, (blocks, 1), 0).astype(F32)
    count = jnp.sum(alive).astype(jnp.int32)
    picks[slots] = count
    index = []
    for j in range(slots):
        index.append(jnp.sum(jnp.where(rank == float(j + 1), number, 0.0)).astype(jnp.int32))

    def copies(j):
        cols = pl.ds(pl.multiple_of(index[j] * block, block), block)
        return (
            pltpu.make_async_copy(
                cold_gate.at[:, cols], w_v.at[j, :, pl.ds(0, block)], w_sem.at[0, j]
            ),
            pltpu.make_async_copy(
                cold_up.at[:, cols], w_v.at[j, :, pl.ds(block, block)], w_sem.at[1, j]
            ),
        )

    for j in range(slots):
        picks[j] = index[j]

        @pl.when(j < count)
        def _():
            for copy in copies(j):
                copy.start()

    loads[1].wait()
    loads[2].wait()
    values = tokens[...].astype(F32)
    scale = lax.rsqrt(jnp.mean(values * values, axis=1, keepdims=True) + 1e-05)
    normed_v[...] = (values * scale * gain[...]).astype(BF16)

    loads[3].wait()
    hidx = hot_index[...] - c * (blocks * block)
    owner = lax.shift_right_arithmetic(hidx, jnp.int32(block.bit_length() - 1))
    inner = jnp.bitwise_and(hidx, jnp.int32(block - 1))
    n = hidx.shape[1]
    by_block = (lax.broadcasted_iota(jnp.int32, (blocks, n), 0) == owner).astype(F32)
    by_unit = (lax.broadcasted_iota(jnp.int32, (block, n), 0) == inner).astype(F32)
    unit_v[...] = 1.0 - lax.dot_general(by_block, by_unit, NT, preferred_element_type=F32)
    chunk = live.shape[0]
    mine = (
        lax.broadcasted_iota(jnp.int32, (chunk, seqs), 1)
        == lax.broadcasted_iota(jnp.int32, (chunk, seqs), 0) + h * chunk
    ).astype(F32)
    seq_mask = lax.dot_general(mine, mask_f, NT, preferred_element_type=F32)
    lane = lax.broadcasted_iota(jnp.int32, (1, blocks), 1)
    for j in range(slots):
        seq_live = jnp.sum(
            jnp.where(lane == index[j], seq_mask, 0.0), axis=1, keepdims=True
        ) * jnp.where(j < count, 1.0, 0.0)
        live[:, pl.ds(j * block, block)] = seq_live * unit_v[pl.ds(index[j], 1), :]

    loads[4].wait()
    loads[5].wait()
    gate_hot = lax.dot_general(normed_v[...], hot_gate[...], NT, preferred_element_type=F32)
    up_hot = lax.dot_general(normed_v[...], hot_up[...], NT, preferred_element_type=F32)
    hidden_hot = (silu(gate_hot) * up_hot).astype(BF16)
    spread = (
        lax.broadcasted_iota(jnp.int32, (rows, rows * n_hot), 1)
        == lax.broadcasted_iota(jnp.int32, (rows, rows * n_hot), 0) + h * rows
    ).astype(BF16)
    out[:, pl.ds(2 * slots * block, rows * n_hot)] = jnp.dot(
        hidden_hot, spread, preferred_element_type=F32
    ).astype(BF16)

    part = normed_v[:, pl.ds(pl.multiple_of(h * feats, feats), feats)]
    for j in range(slots):
        cols = pl.ds(2 * j * block, 2 * block)

        @pl.when(j < count)
        def _():
            for copy in copies(j):
                copy.wait()
            out[:, cols] = jnp.dot(part, w_v[j], preferred_element_type=F32).astype(BF16)

        @pl.when(j >= count)
        def _():
            out[:, cols] = jnp.zeros((seqs, 2 * block), BF16)


def hidden_kernel(parts, live, out, *, slots, block, n_hot):
    chunk = live.shape[0]
    total = parts[pl.ds(0, chunk), :].astype(F32)
    for src in range(1, n_hot):
        total = total + parts[pl.ds(src * chunk, chunk), :].astype(F32)
    pieces = []
    for j in range(slots):
        gate = total[:, 2 * j * block : (2 * j + 1) * block]
        up = total[:, (2 * j + 1) * block : (2 * j + 2) * block]
        pieces.append((silu(gate) * up * live[:, pl.ds(j * block, block)]).astype(BF16))
    pieces.append(total[:, 2 * slots * block :].astype(BF16))
    hidden = jnp.concatenate(pieces, axis=1)
    for dst in range(n_hot):
        out[pl.ds(dst * chunk, chunk), :] = hidden


def down_kernel(picks, hidden, hot_rows, cold_down, own, *rest, slots, block):
    sends, (total, w, sem) = rest[:-3], rest[-3:]
    count = picks[slots]
    group = 2 if slots % 2 == 0 else 1

    def copy(j):
        rows = pl.ds(pl.multiple_of(picks[j] * block, block), block)
        return pltpu.make_async_copy(cold_down.at[rows], w.at[pl.ds(j * block, block)], sem.at[j])

    for j in range(slots):

        @pl.when(j < count)
        def _():
            copy(j).start()

        @pl.when(j >= count)
        def _():
            w[pl.ds(j * block, block), :] = jnp.zeros((block, w.shape[1]), BF16)

    base = slots * block
    total[...] = jnp.dot(
        hidden[:, pl.ds(base, hot_rows.shape[0])], hot_rows[...], preferred_element_type=F32
    )
    for first in range(0, slots, group):

        @pl.when(first < count)
        def _():
            for j in range(first, first + group):

                @pl.when(j < count)
                def _():
                    copy(j).wait()

            rows = pl.ds(first * block, group * block)
            total[...] += jnp.dot(hidden[:, rows], w[rows, :], preferred_element_type=F32)

    c = lax.axis_index("cold")
    cols = own.shape[1]

    def piece(k):
        if cols % 128 == 0:
            return total[:, pl.ds(pl.multiple_of(k * cols, cols), cols)]
        value = jnp.zeros((total.shape[0], cols), F32)
        for i in range(total.shape[1] // cols):
            value = jnp.where(k == i, total[:, i * cols : (i + 1) * cols], value)
        return value

    own[...] = piece(c)
    for k, send in enumerate(sends):
        send[...] = piece(jnp.bitwise_xor(c, k + 1)).astype(send.dtype)


def in_vmem(value):
    return pltpu.with_memory_space_constraint(value, pltpu.VMEM)


def in_hbm(value):
    return pltpu.with_memory_space_constraint(value, pltpu.HBM)


def on_device(
    tokens, norm_gain, hot_gate, hot_up, hot_down, hot_index,
    cold_gate, cold_up, cold_down, block_mask, *, n_hot, n_cold,
):
    seqs, width = tokens.shape
    feats, units = cold_gate.shape
    blocks = block_mask.shape[1]
    block = units // blocks
    slots = blocks // 2
    rows = hot_gate.shape[0]
    chunk = seqs // n_hot
    hot_lanes = rows * n_hot
    cols = cold_down.shape[1]

    hot_rows = lax.all_to_all(hot_down, "hot", split_axis=1, concat_axis=0, tiled=True)

    parts, live, picks = pl.pallas_call(
        functools.partial(partial_kernel, slots=slots, block=block, n_hot=n_hot),
        name="partial",
        compiler_params=limit(20),
        in_specs=[ANY] * 8,
        out_specs=[VMEM, VMEM, SMEM],
        out_shape=[
            pltpu.VMEM((seqs, 2 * slots * block + hot_lanes), BF16),
            pltpu.VMEM((chunk, slots * block), F32),
            jax.ShapeDtypeStruct((slots + 1,), jnp.int32),
        ],
        scratch_shapes=[
            pltpu.VMEM((seqs, width), BF16),
            pltpu.VMEM((1, width), F32),
            pltpu.VMEM((rows, width), BF16),
            pltpu.VMEM((rows, width), BF16),
            pltpu.VMEM((1, hot_index.shape[0]), jnp.int32),
            pltpu.VMEM((blocks, seqs), jnp.int32),
            pltpu.VMEM((seqs, width), BF16),
            pltpu.VMEM((blocks, block), F32),
            pltpu.VMEM((slots, feats, 2 * block), BF16),
            pltpu.SemaphoreType.DMA((6,)),
            pltpu.SemaphoreType.DMA((2, slots)),
        ],
    )(*(in_hbm(value) for value in (
        tokens, norm_gain[None, :], hot_gate, hot_up, hot_index[None, :],
        block_mask.T, cold_gate, cold_up,
    )))
    parts, hot_rows = lax.optimization_barrier((parts, hot_rows))
    parts = lax.all_to_all(parts, "hot", split_axis=0, concat_axis=0, tiled=True)
    hidden = pl.pallas_call(
        functools.partial(hidden_kernel, slots=slots, block=block, n_hot=n_hot),
        name="hidden",
        compiler_params=limit(8),
        in_specs=[VMEM, VMEM],
        out_specs=VMEM,
        out_shape=pltpu.VMEM((seqs, slots * block + hot_lanes), BF16),
    )(in_vmem(parts), in_vmem(live))
    hidden = lax.all_to_all(hidden, "hot", split_axis=0, concat_axis=0, tiled=True)
    piece = (seqs, cols // n_cold)
    own, *sends = pl.pallas_call(
        functools.partial(down_kernel, slots=slots, block=block),
        name="down",
        compiler_params=limit(8),
        in_specs=[SMEM, VMEM, VMEM, ANY],
        out_specs=[VMEM] * n_cold,
        out_shape=[pltpu.VMEM(piece, F32)] + [pltpu.VMEM(piece, BF16)] * (n_cold - 1),
        scratch_shapes=[
            pltpu.VMEM((seqs, cols), F32),
            pltpu.VMEM((slots * block, cols), BF16),
            pltpu.SemaphoreType.DMA((slots,)),
        ],
    )(picks, in_vmem(hidden), in_vmem(hot_rows), in_hbm(cold_down))
    for k, send in enumerate(sends):
        got = lax.ppermute(send, "cold", [(i, i ^ (k + 1)) for i in range(n_cold)])
        own = own + got.astype(F32)
    return own.astype(BF16)


def solution(mesh):
    in_specs = (
        P(),
        P(),
        P(("hot", "cold"), None),
        P(("hot", "cold"), None),
        P(("hot", "cold"), None),
        P(),
        P("hot", "cold"),
        P("hot", "cold"),
        P("cold", "hot"),
        P(None, "cold"),
    )

    def body(*args):
        return on_device(*args, n_hot=mesh.shape["hot"], n_cold=mesh.shape["cold"])

    return jax.shard_map(
        body, mesh=mesh, in_specs=in_specs, out_specs=P(None, ("hot", "cold")), check_vma=False
    )
```

time: 65.5 us -> 54.4 us (0.83)
  waiting for transfers between devices: 20.9 us -> 7.42 us
  blocking collectives: 20 us -> 28.2 us
  Pallas kernels: 10.5 us -> 6.86 us
  starting transfers between devices: 11.5 us -> 9.23 us
    all_to_all x1 -> x0, waiting for transfers between devices: 13.5 us -> none  [on_device(): lax.all_to_all(parts, 'hot', split_axis=0, concat_axis=0, tiled=True)]
    all_to_all x1, blocking collectives: 7.9 us -> 16.5 us  [on_device(): lax.all_to_all(parts, 'hot', split_axis=0, concat_axis=0, tiled=True)]
    all_to_all x1 -> x0, starting transfers between devices: 7.32 us -> none  [on_device(): lax.all_to_all(parts, 'hot', split_axis=0, concat_axis=0, tiled=True)]
    ppermute x0 -> x3, waiting for transfers between devices: none -> 3.12 us  [on_device(): got = lax.ppermute(send, 'cold', [(i, i ^ k + 1) for i in range(n_cold)])]
    all_to_all x1, starting transfers between devices: 4.21 us -> 7.31 us  [on_device(): lax.all_to_all(hot_down, 'hot', split_axis=1, concat_axis=0, tiled=True)]
    all_to_all x1, waiting for transfers between devices: 7.38 us -> 4.3 us  [on_device(): lax.all_to_all(hot_down, 'hot', split_axis=1, concat_axis=0, tiled=True)]
    ppermute x0 -> x3, starting transfers between devices: none -> 1.92 us  [on_device(): got = lax.ppermute(send, 'cold', [(i, i ^ k + 1) for i in range(n_cold)])]
    pallas_call x1, Pallas kernels: 1.81 us -> 0.09 us  [on_device(): pl.pallas_call(functools.partial(hidden_kernel, slots=slots, block=block,...]
  transfers between devices with their start and end apart: 2 -> 4, of which waited for: 2 -> 3; matrix products, arithmetic and copies ran while one was open for 1% -> 0% of each run, Pallas kernels for 3% -> 9%
where the time goes in v2:
time: 54.4 us; the launch traced here: 54 us
  blocking collectives  28.2 us (52%)
  starting transfers between devices  9.23 us (17%)
  waiting for transfers between devices  7.42 us (14%)
  Pallas kernels  6.86 us (13%)
  local copies, waits for them, and re-layouts  1.67 us (3%)
  other arithmetic  0.63 us (1%)
    all_to_all x1, blocking collectives, on_device(): lax.all_to_all(parts, 'hot', split_axis=0, concat_axis=0, tiled=True)  16.5 us
    all_to_all x1, blocking collectives, on_device(): lax.all_to_all(hidden, 'hot', split_axis=0, concat_axis=0, tiled=True)  11.6 us
    all_to_all x1, starting transfers between devices, on_device(): lax.all_to_all(hot_down, 'hot', split_axis=1, concat_axis=0, tiled=True)  7.31 us
    pallas_call x1, Pallas kernels, on_device(): pl.pallas_call(functools.partial(partial_kernel, slots=slots, block=block...  4.61 us
    all_to_all x1, waiting for transfers between devices, on_device(): lax.all_to_all(hot_down, 'hot', split_axis=1, concat_axis=0, tiled=True)  4.3 us
    ppermute x3, waiting for transfers between devices, on_device(): got = lax.ppermute(send, 'cold', [(i, i ^ k + 1) for i in range(n_cold)])  3.12 us
    pallas_call x1, Pallas kernels, on_device(): pl.pallas_call(functools.partial(down_kernel, slots=slots, block=block),...  2.16 us
    ppermute x3, starting transfers between devices, on_device(): got = lax.ppermute(send, 'cold', [(i, i ^ k + 1) for i in range(n_cold)])  1.92 us
  transfers between devices with their start and end apart: 4, of which 3 were waited for; matrix products, arithmetic and copies ran while one was open for 0% of the time, Pallas kernels for 9%

profile of v2, /device:TPU:0, one launch (start us, length us, event | category | flops | bytes accessed | tf_op | source)
XLA Modules:
  0.0 54.0 jit_solution(5438129357627469746)
XLA Ops:
  0.0 1.7 %copy.14 = bf16[2,8,8,1024]{3,2,0,1:T(8,128)(2,1)} copy(bf16[2,8,8,1024]{3,2,1,0:T(8,128)(2,1)} %bitcast.19) | data formatting | bytes 524288 | tf_op jit(solution)/shard_map/all_to_all | solution.py:228
  1.7 7.3 %all-to-all-start = ((bf16[16,8,1024]{2,0,1:T(8,128)(2,1)}), bf16[16,8,1024]{2,0,1:T(8,128)(2,1)S(1)}, u32[]{:S(2)}, u32[]{:S(2)}) async-start(bf16[16,8,1024]{2,0,1:T(8,128)(2,1)} %bitcast.13), calls=%async_computation | async-start | bytes 524288 | tf_op jit(solution)/shard_map/all_to_all | solution.py:228
  9.0 4.6 %partial.1 = (bf16[64,3712]{1,0:T(8,128)(2,1)S(1)}, f32[8,1792]{1,0:T(8,128)S(1)}, s32[15]{0:T(128)S(1)}) custom-call(bf16[64,8192]{1,0:T(8,128)(2,1)} %tokens_hbm.1, f32[1,8192]{1,0:T(1,128)} %bitcast.20, bf16[16,8192]{1,0:T(8,128)(2,1)} %hot_gate_hbm.1, bf16[16,8192]{1,0:T(8,128)(2,1)} %hot_up_hbm.1, s32[1,512]{1,0:T(1,128)} %bitcast.22, ...), custom_call_target="tpu_custom_call" | custom-call | tf_op jit(solution)/shard_map/partial/pallas_call | solution.py:230
  13.6 4.3 %all-to-all-done = bf16[16,8,1024]{2,0,1:T(8,128)(2,1)S(1)} async-done(((bf16[16,8,1024]{2,0,1:T(8,128)(2,1)}), bf16[16,8,1024]{2,0,1:T(8,128)(2,1)S(1)}, u32[]{:S(2)}, u32[]{:S(2)}) %all-to-all-start) | async-done | bytes 262176 | tf_op jit(solution)/shard_map/all_to_all | solution.py:228
  17.9 16.5 %all_to_all.41 = bf16[8,8,3712]{2,1,0:T(8,128)(2,1)S(1)} all-to-all(bf16[8,8,3712]{2,1,0:T(8,128)(2,1)S(1)} %bitcast.18), channel_id=1, replica_groups=mesh['hot'=8,'cold'=4] {'hot'}, dimensions={0} | all-to-all | bytes 950272 | tf_op jit(solution)/shard_map/all_to_all | solution.py:259
  34.4 0.1 hidden.1
  34.5 11.6 %all_to_all.42 = bf16[8,8,1920]{2,1,0:T(8,128)(2,1)S(1)} all-to-all(bf16[8,8,1920]{2,1,0:T(8,128)(2,1)S(1)} %bitcast.17), channel_id=1, replica_groups=mesh['hot'=8,'cold'=4] {'hot'}, dimensions={0} | all-to-all | bytes 491520 | tf_op jit(solution)/shard_map/all_to_all | solution.py:268
  46.2 2.2 %down.1 = (f32[64,256]{1,0:T(8,128)S(1)}, bf16[64,256]{1,0:T(8,128)(2,1)S(1)}, bf16[64,256]{1,0:T(8,128)(2,1)S(1)}, bf16[64,256]{1,0:T(8,128)(2,1)S(1)}) custom-call(s32[15]{0:T(128)S(1)} %get-tuple-element.14.picks, bf16[64,1920]{1,0:T(8,128)(2,1)S(1)} %bitcast.16, bf16[128,1024]{1,0:T(8,128)(2,1)S(1)} %bitcast.15, bf16[3584,1024]{1,0:T(8,128)(2,1)} %cold_down.1), custom_call_target="tpu_custom_call" | custom-call | tf_op jit(solution)/shard_map/down/pallas_call | solution.py:270
  48.3 0.1 collective-permute-start
  48.4 1.6 %collective-permute-start.1 = (bf16[64,256]{1,0:T(8,128)(2,1)S(1)}, bf16[64,256]{1,0:T(8,128)(2,1)S(1)}, u32[]{:S(2)}, u32[]{:S(2)}) collective-permute-start(bf16[64,256]{1,0:T(8,128)(2,1)S(1)} %get-tuple-element.21), channel_id=1, source_target_pairs={{0,2},{1,3},{2,0},{3,1},{4,6},{5,7},{6,4},{7,5},{8,10},{9,11},{10,... | collective-permute-start | bytes 98312 | tf_op jit(solution)/shard_map/ppermute | solution.py:284
  50.0 0.2 collective-permute-start.2
  50.3 0.0 collective-permute-done
  50.3 2.1 %collective-permute-done.1 = bf16[64,256]{1,0:T(8,128)(2,1)S(1)} collective-permute-done((bf16[64,256]{1,0:T(8,128)(2,1)S(1)}, bf16[64,256]{1,0:T(8,128)(2,1)S(1)}, u32[]{:S(2)}, u32[]{:S(2)}) %collective-permute-start.1) | collective-permute-done | bytes 32800 | tf_op jit(solution)/shard_map/ppermute | solution.py:284
  52.4 1.0 %collective-permute-done.2 = bf16[64,256]{1,0:T(8,128)(2,1)S(1)} collective-permute-done((bf16[64,256]{1,0:T(8,128)(2,1)S(1)}, bf16[64,256]{1,0:T(8,128)(2,1)S(1)}, u32[]{:S(2)}, u32[]{:S(2)}) %collective-permute-start.2) | collective-permute-done | bytes 32800 | tf_op jit(solution)/shard_map/ppermute | solution.py:284
  53.4 0.6 %add_convert_fusion = bf16[64,256]{1,0:T(8,128)(2,1)} fusion(bf16[64,256]{1,0:T(8,128)(2,1)S(1)} %collective-permute-done.2, bf16[64,256]{1,0:T(8,128)(2,1)S(1)} %collective-permute-done.1, f32[64,256]{1,0:T(8,128)S(1)} %get-tuple-element.19, bf16[64,256]{1,0:T(8,128)(2,1)S(1)} %collective-permute-done), kind=kLoop, calls=%fused_computation.1 | loop fusion | flops 114688 | bytes 196608 | tf_op jit(solution)/shard_map/convert_element_type | solution.py:286
Async XLA Ops:
  1.7 16.2 %all-to-all-start = ((bf16[16,8,1024]{2,0,1:T(8,128)(2,1)}), bf16[16,8,1024]{2,0,1:T(8,128)(2,1)S(1)}, u32[]{:S(2)}, u32[]{:S(2)}) async-start(bf16[16,8,1024]{2,0,1:T(8,128)(2,1)} %bitcast.13), calls=%async_computation | async-start | bytes 524288 | tf_op jit(solution)/shard_map/all_to_all | solution.py:228
  48.3 1.9 %collective-permute-start = (bf16[64,256]{1,0:T(8,128)(2,1)S(1)}, bf16[64,256]{1,0:T(8,128)(2,1)S(1)}, u32[]{:S(2)}, u32[]{:S(2)}) collective-permute-start(bf16[64,256]{1,0:T(8,128)(2,1)S(1)} %get-tuple-element.20), channel_id=1, source_target_pairs={{0,1},{1,0},{2,3},{3,2},{4,5},{5,4},{6,7},{7,6},{8,9},{9,8},{10,11... | collective-permute-start | bytes 98312 | tf_op jit(solution)/shard_map/ppermute | solution.py:284
  48.4 4.0 %collective-permute-start.1 = (bf16[64,256]{1,0:T(8,128)(2,1)S(1)}, bf16[64,256]{1,0:T(8,128)(2,1)S(1)}, u32[]{:S(2)}, u32[]{:S(2)}) collective-permute-start(bf16[64,256]{1,0:T(8,128)(2,1)S(1)} %get-tuple-element.21), channel_id=1, source_target_pairs={{0,2},{1,3},{2,0},{3,1},{4,6},{5,7},{6,4},{7,5},{8,10},{9,11},{10,... | collective-permute-start | bytes 98312 | tf_op jit(solution)/shard_map/ppermute | solution.py:284
  50.0 3.4 %collective-permute-start.2 = (bf16[64,256]{1,0:T(8,128)(2,1)S(1)}, bf16[64,256]{1,0:T(8,128)(2,1)S(1)}, u32[]{:S(2)}, u32[]{:S(2)}) collective-permute-start(bf16[64,256]{1,0:T(8,128)(2,1)S(1)} %get-tuple-element.22), channel_id=1, source_target_pairs={{0,3},{1,2},{2,1},{3,0},{4,7},{5,6},{6,5},{7,4},{8,11},{9,10},{10,... | collective-permute-start | bytes 98312 | tf_op jit(solution)/shard_map/ppermute | solution.py:284

commit v3 on v2

--- a/solution.py
+++ b/solution.py
@@ -7,7 +7,6 @@
 from jax.experimental.pallas import tpu as pltpu
 from jax.sharding import PartitionSpec as P
 
-
 F32 = jnp.float32
 BF16 = jnp.bfloat16
 ANY = pl.BlockSpec(memory_space=pl.ANY)
@@ -26,15 +25,18 @@
 
 def partial_kernel(
     tokens_hbm, gain_hbm, hot_gate_hbm, hot_up_hbm, hot_index_hbm, mask_hbm, cold_gate, cold_up,
-    out, live, picks,
-    tokens, gain, hot_gate, hot_up, hot_index, mask, normed_v, unit_v, w_v, in_sem, w_sem,
-    *, slots, block, n_hot,
+    hot_down,
+    out, few, live, picks, flag,
+    tokens, gain, hot_w, hot_index, mask, normed_v, unit_v, w_v, in_sem, w_sem, row_sem,
+    *, slots, block, n_hot, fold,
 ):
+    rows = hot_gate_hbm.shape[0]
     loads = [
         pltpu.make_async_copy(source, target, in_sem.at[i])
         for i, (source, target) in enumerate((
             (mask_hbm, mask), (tokens_hbm, tokens), (gain_hbm, gain),
-            (hot_index_hbm, hot_index), (hot_gate_hbm, hot_gate), (hot_up_hbm, hot_up),
+            (hot_index_hbm, hot_index), (hot_gate_hbm, hot_w.at[pl.ds(0, rows)]),
+            (hot_up_hbm, hot_w.at[pl.ds(rows, rows)]),
         ))
     ]
     for load in loads:
@@ -43,9 +45,12 @@
     seqs = tokens.shape[0]
     feats = cold_gate.shape[0]
     blocks = mask.shape[0]
-    rows = hot_gate.shape[0]
     h = lax.axis_index("hot")
     c = lax.axis_index("cold")
+    start = rows * n_hot
+    cols = hot_down.shape[1] // n_hot
+    chunk = live.shape[0]
+    base = start + (rows // chunk * cols if fold else 0)
     mask_f = mask[...].astype(F32)
     alive = jnp.max(mask_f, axis=1, keepdims=True)
     tri = (
@@ -57,6 +62,7 @@
     number = lax.broadcasted_iota(jnp.int32, (blocks, 1), 0).astype(F32)
     count = jnp.sum(alive).astype(jnp.int32)
     picks[slots] = count
+    flag[0] = jnp.where(count <= (few.shape[1] - base) // (2 * block), 1, 0)
     index = []
     for j in range(slots):
         index.append(jnp.sum(jnp.where(rank == float(j + 1), number, 0.0)).astype(jnp.int32))
@@ -80,11 +86,31 @@
             for copy in copies(j):
                 copy.start()
 
+    row_copies = []
+    if fold:
+        for dst in range(n_hot):
+            for i in range(rows // chunk):
+                row_copies.append(pltpu.make_async_copy(
+                    hot_down.at[pl.ds(i * chunk, chunk), pl.ds(dst * cols, cols)],
+                    out.at[pl.ds(dst * chunk, chunk), pl.ds(start + i * cols, cols)],
+                    row_sem.at[dst, i],
+                ))
+    for copy in row_copies:
+        copy.start()
+
     loads[1].wait()
     loads[2].wait()
-    values = tokens[...].astype(F32)
-    scale = lax.rsqrt(jnp.mean(values * values, axis=1, keepdims=True) + 1e-05)
-    normed_v[...] = (values * scale * gain[...]).astype(BF16)
+    width = tokens.shape[1]
+    squares = jnp.zeros((seqs, block), F32)
+    for first in range(0, width, block):
+        values = tokens[:, pl.ds(first, block)].astype(F32)
+        squares += values * values
+    scale = lax.rsqrt(jnp.sum(squares, axis=1, keepdims=True) / width + 1e-05)
+    scale = jnp.broadcast_to(scale, (seqs, block))
+    for first in range(0, width, block):
+        lanes = pl.ds(first, block)
+        values = tokens[:, lanes].astype(F32) * scale * gain[:, lanes]
+        normed_v[:, lanes] = values.astype(BF16)
 
     loads[3].wait()
     hidx = hot_index[...] - c * (blocks * block)
@@ -94,7 +120,6 @@
     by_block = (lax.broadcasted_iota(jnp.int32, (blocks, n), 0) == owner).astype(F32)
     by_unit = (lax.broadcasted_iota(jnp.int32, (block, n), 0) == inner).astype(F32)
     unit_v[...] = 1.0 - lax.dot_general(by_block, by_unit, NT, preferred_element_type=F32)
-    chunk = live.shape[0]
     mine = (
         lax.broadcasted_iota(jnp.int32, (chunk, seqs), 1)
         == lax.broadcasted_iota(jnp.int32, (chunk, seqs), 0) + h * chunk
@@ -109,51 +134,72 @@
 
     loads[4].wait()
     loads[5].wait()
-    gate_hot = lax.dot_general(normed_v[...], hot_gate[...], NT, preferred_element_type=F32)
-    up_hot = lax.dot_general(normed_v[...], hot_up[...], NT, preferred_element_type=F32)
-    hidden_hot = (silu(gate_hot) * up_hot).astype(BF16)
+    both = lax.dot_general(normed_v[...], hot_w[...], NT, preferred_element_type=F32)
+    hidden_hot = (silu(both[:, :rows]) * both[:, rows:]).astype(BF16)
     spread = (
         lax.broadcasted_iota(jnp.int32, (rows, rows * n_hot), 1)
         == lax.broadcasted_iota(jnp.int32, (rows, rows * n_hot), 0) + h * rows
     ).astype(BF16)
-    out[:, pl.ds(2 * slots * block, rows * n_hot)] = jnp.dot(
+    out[:, pl.ds(0, rows * n_hot)] = jnp.dot(
         hidden_hot, spread, preferred_element_type=F32
     ).astype(BF16)
 
     part = normed_v[:, pl.ds(pl.multiple_of(h * feats, feats), feats)]
     for j in range(slots):
-        cols = pl.ds(2 * j * block, 2 * block)
+        lanes = pl.ds(base + 2 * j * block, 2 * block)
 
         @pl.when(j < count)
         def _():
             for copy in copies(j):
                 copy.wait()
-            out[:, cols] = jnp.dot(part, w_v[j], preferred_element_type=F32).astype(BF16)
+            out[:, lanes] = jnp.dot(part, w_v[j], preferred_element_type=F32).astype(BF16)
 
         @pl.when(j >= count)
         def _():
-            out[:, cols] = jnp.zeros((seqs, 2 * block), BF16)
-
-
-def hidden_kernel(parts, live, out, *, slots, block, n_hot):
+            out[:, lanes] = jnp.zeros((seqs, 2 * block), BF16)
+
+    for copy in row_copies:
+        copy.wait()
+
+    @pl.when(count <= (few.shape[1] - base) // (2 * block))
+    def _():
+        few[...] = out[:, pl.ds(0, few.shape[1])]
+
+
+def hidden_kernel(parts, live, out, *hot_rows, slots, block, n_hot, hot_lanes):
     chunk = live.shape[0]
-    total = parts[pl.ds(0, chunk), :].astype(F32)
-    for src in range(1, n_hot):
-        total = total + parts[pl.ds(src * chunk, chunk), :].astype(F32)
+    base = parts.shape[1] - 2 * slots * block
+
+    def total(start, width):
+        lanes = pl.ds(start, width)
+        value = parts[pl.ds(0, chunk), lanes].astype(F32)
+        for src in range(1, n_hot):
+            value = value + parts[pl.ds(src * chunk, chunk), lanes].astype(F32)
+        return value
+
+    both = total(base, 2 * slots * block)
     pieces = []
     for j in range(slots):
-        gate = total[:, 2 * j * block : (2 * j + 1) * block]
-        up = total[:, (2 * j + 1) * block : (2 * j + 2) * block]
+        gate = both[:, 2 * j * block : (2 * j + 1) * block]
+        up = both[:, (2 * j + 1) * block : (2 * j + 2) * block]
         pieces.append((silu(gate) * up * live[:, pl.ds(j * block, block)]).astype(BF16))
-    pieces.append(total[:, 2 * slots * block :].astype(BF16))
+    pieces.append(total(0, hot_lanes).astype(BF16))
     hidden = jnp.concatenate(pieces, axis=1)
     for dst in range(n_hot):
         out[pl.ds(dst * chunk, chunk), :] = hidden
+    for rows in hot_rows:
+        cols = rows.shape[1]
+        each = hot_lanes // n_hot // chunk
+        for src in range(n_hot):
+            for i in range(each):
+                rows[pl.ds((src * each + i) * chunk, chunk), :] = parts[
+                    pl.ds(src * chunk, chunk), pl.ds(hot_lanes + i * cols, cols)
+                ]
 
 
 def down_kernel(picks, hidden, hot_rows, cold_down, own, *rest, slots, block):
     sends, (total, w, sem) = rest[:-3], rest[-3:]
-    count = picks[slots]
+    count = picks[picks.shape[0] - 1]
     group = 2 if slots % 2 == 0 else 1
 
     def copy(j):
@@ -225,24 +271,30 @@
     hot_lanes = rows * n_hot
     cols = cold_down.shape[1]
 
-    hot_rows = lax.all_to_all(hot_down, "hot", split_axis=1, concat_axis=0, tiled=True)
-
-    parts, live, picks = pl.pallas_call(
-        functools.partial(partial_kernel, slots=slots, block=block, n_hot=n_hot),
+    fold = chunk % 8 == 0 and rows % chunk == 0
+    row_lanes = rows // chunk * cols if fold else 0
+    shared = hot_lanes + row_lanes
+    few = max(2, slots // 6 * 2)
+
+    parts, few_parts, live, picks, flag = pl.pallas_call(
+        functools.partial(
+            partial_kernel, slots=slots, block=block, n_hot=n_hot, fold=fold
+        ),
         name="partial",
         compiler_params=limit(20),
-        in_specs=[ANY] * 8,
-        out_specs=[VMEM, VMEM, SMEM],
+        in_specs=[ANY] * 9,
+        out_specs=[VMEM, VMEM, VMEM, SMEM, SMEM],
         out_shape=[
-            pltpu.VMEM((seqs, 2 * slots * block + hot_lanes), BF16),
+            pltpu.VMEM((seqs, shared + 2 * slots * block), BF16),
+            pltpu.VMEM((seqs, shared + 2 * few * block), BF16),
             pltpu.VMEM((chunk, slots * block), F32),
-            jax.ShapeDtypeStruct((slots + 1,), jnp.int32),
+            pltpu.SMEM((slots + 1,), jnp.int32),
+            pltpu.SMEM((1,), jnp.int32),
         ],
         scratch_shapes=[
             pltpu.VMEM((seqs, width), BF16),
             pltpu.VMEM((1, width), F32),
-            pltpu.VMEM((rows, width), BF16),
-            pltpu.VMEM((rows, width), BF16),
+            pltpu.VMEM((2 * rows, width), BF16),
             pltpu.VMEM((1, hot_index.shape[0]), jnp.int32),
             pltpu.VMEM((blocks, seqs), jnp.int32),
             pltpu.VMEM((seqs, width), BF16),
@@ -250,36 +302,54 @@
             pltpu.VMEM((slots, feats, 2 * block), BF16),
             pltpu.SemaphoreType.DMA((6,)),
             pltpu.SemaphoreType.DMA((2, slots)),
+            pltpu.SemaphoreType.DMA((n_hot, max(1, rows // chunk))),
         ],
     )(*(in_hbm(value) for value in (
         tokens, norm_gain[None, :], hot_gate, hot_up, hot_index[None, :],
-        block_mask.T, cold_gate, cold_up,
+        block_mask.T, cold_gate, cold_up, hot_down,
     )))
-    parts, hot_rows = lax.optimization_barrier((parts, hot_rows))
-    parts = lax.all_to_all(parts, "hot", split_axis=0, concat_axis=0, tiled=True)
-    hidden = pl.pallas_call(
-        functools.partial(hidden_kernel, slots=slots, block=block, n_hot=n_hot),
-        name="hidden",
-        compiler_params=limit(8),
-        in_specs=[VMEM, VMEM],
-        out_specs=VMEM,
-        out_shape=pltpu.VMEM((seqs, slots * block + hot_lanes), BF16),
-    )(in_vmem(parts), in_vmem(live))
-    hidden = lax.all_to_all(hidden, "hot", split_axis=0, concat_axis=0, tiled=True)
-    piece = (seqs, cols // n_cold)
-    own, *sends = pl.pallas_call(
-        functools.partial(down_kernel, slots=slots, block=block),
-        name="down",
-        compiler_params=limit(8),
-        in_specs=[SMEM, VMEM, VMEM, ANY],
-        out_specs=[VMEM] * n_cold,
-        out_shape=[pltpu.VMEM(piece, F32)] + [pltpu.VMEM(piece, BF16)] * (n_cold - 1),
-        scratch_shapes=[
-            pltpu.VMEM((seqs, cols), F32),
-            pltpu.VMEM((slots * block, cols), BF16),
-            pltpu.SemaphoreType.DMA((slots,)),
-        ],
-    )(picks, in_vmem(hidden), in_vmem(hot_rows), in_hbm(cold_down))
+
+    def middle(slots, parts, live, picks, hot_down, cold_down):
+        parts = lax.all_to_all(parts, "hot", split_axis=0, concat_axis=0, tiled=True)
+        hidden, *moved = pl.pallas_call(
+            functools.partial(
+                hidden_kernel, slots=slots, block=block, n_hot=n_hot, hot_lanes=hot_lanes
+            ),
+            name="hidden",
+            compiler_params=limit(8),
+            in_specs=[VMEM, VMEM],
+            out_specs=[VMEM] * (1 + fold),
+            out_shape=[
+                pltpu.VMEM((seqs, slots * block + hot_lanes), BF16),
+                pltpu.VMEM((hot_lanes, cols), BF16),
+            ][: 1 + fold],
+        )(in_vmem(parts), in_vmem(live))
+        if fold:
+            hot_rows = moved[0]
+        else:
+            hot_rows = lax.all_to_all(hot_down, "hot", split_axis=1, concat_axis=0, tiled=True)
+        hidden = lax.all_to_all(hidden, "hot", split_axis=0, concat_axis=0, tiled=True)
+        piece = (seqs, cols // n_cold)
+        return tuple(pl.pallas_call(
+            functools.partial(down_kernel, slots=slots, block=block),
+            name="down",
+            compiler_params=limit(8),
+            in_specs=[SMEM, VMEM, VMEM, ANY],
+            out_specs=[VMEM] * n_cold,
+            out_shape=[pltpu.VMEM(piece, F32)] + [pltpu.VMEM(piece, BF16)] * (n_cold - 1),
+            scratch_shapes=[
+                pltpu.VMEM((seqs, cols), F32),
+                pltpu.VMEM((slots * block, cols), BF16),
+                pltpu.SemaphoreType.DMA((slots,)),
+            ],
+        )(pltpu.with_memory_space_constraint(picks, pltpu.SMEM), in_vmem(hidden), in_vmem(hot_rows), in_hbm(cold_down)))
+
+    own, *sends = lax.cond(
+        flag[0] > 0,
+        lambda parts, few_parts, *rest: middle(few, few_parts, *rest),
+        lambda parts, few_parts, *rest: middle(slots, parts, *rest),
+        parts, few_parts, live, picks, hot_down, cold_down,
+    )
     for k, send in enumerate(sends):
         got = lax.ppermute(send, "cold", [(i, i ^ (k + 1)) for i in range(n_cold)])
         own = own + got.astype(F32)

time: 54.4 us -> 46.6 us (0.86)
  waiting for transfers between devices: 7.42 us -> 3.66 us
  starting transfers between devices: 9.23 us -> 6.99 us
  local copies, waits for them, and re-layouts: 1.67 us -> 0 us
  Pallas kernels: 6.86 us -> 5.46 us
  blocking collectives: 28.2 us -> 29.5 us
    all_to_all x1 -> x0, starting transfers between devices: 7.31 us -> none  [on_device(): lax.all_to_all(hot_down, 'hot', split_axis=1, concat_axis=0, tiled=True)]
    ppermute x3, starting transfers between devices: 1.92 us -> 6.99 us  [on_device(): got = lax.ppermute(send, 'cold', [(i, i ^ k + 1) for i in range(n_cold)])]
    all_to_all x1 -> x0, waiting for transfers between devices: 4.3 us -> none  [on_device(): lax.all_to_all(hot_down, 'hot', split_axis=1, concat_axis=0, tiled=True)]
    all_to_all x1 -> x0, local copies, waits for them, and re-layouts: 1.67 us -> none  [on_device(): lax.all_to_all(hot_down, 'hot', split_axis=1, concat_axis=0, tiled=True)]
    all_to_all x2, blocking collectives: 28.2 us -> 29.5 us  [the longest x1 19.4 us: middle(): lax.all_to_all(parts, 'hot', split_axis=0, concat_axis=0, tiled=True)]
    pallas_call x2, Pallas kernels: 2.25 us -> 1.55 us  [the longest x1 1.51 us: middle(): pl.pallas_call(functools.partial(down_kernel, slots=slots, block=block),...]
    pallas_call x1, Pallas kernels: 4.61 us -> 3.92 us  [on_device(): pl.pallas_call(functools.partial(partial_kernel, slots=slots, block=block...]
  transfers between devices with their start and end apart: 4 -> 3, of which waited for: 3 -> 2; matrix products, arithmetic and copies ran while one was open for 0% -> 0% of each run, Pallas kernels for 9% -> 0%
where the time goes in v3:
time: 46.6 us; the launch traced here: 46.3 us
  blocking collectives  29.5 us (63%)
  starting transfers between devices  6.99 us (15%)
  Pallas kernels  5.46 us (12%)
  waiting for transfers between devices  3.66 us (8%)
  other arithmetic  0.63 us (1%)
    all_to_all x1, blocking collectives, middle(): lax.all_to_all(parts, 'hot', split_axis=0, concat_axis=0, tiled=True)  19.4 us
    all_to_all x1, blocking collectives, middle(): lax.all_to_all(hidden, 'hot', split_axis=0, concat_axis=0, tiled=True)  10.1 us
    ppermute x3, starting transfers between devices, on_device(): got = lax.ppermute(send, 'cold', [(i, i ^ k + 1) for i in range(n_cold)])  6.99 us
    pallas_call x1, Pallas kernels, on_device(): pl.pallas_call(functools.partial(partial_kernel, slots=slots, block=block...  3.92 us
    ppermute x3, waiting for transfers between devices, on_device(): got = lax.ppermute(send, 'cold', [(i, i ^ k + 1) for i in range(n_cold)])  3.66 us
    pallas_call x1, Pallas kernels, middle(): pl.pallas_call(functools.partial(down_kernel, slots=slots, block=block),...  1.51 us
  transfers between devices with their start and end apart: 3, of which 2 were waited for; matrix products, arithmetic and copies ran while one was open for 0% of the time, Pallas kernels for 0%

profile of v3, /device:TPU:0, one launch (start us, length us, event | category | flops | bytes accessed | tf_op | source)
XLA Modules:
  0.0 46.3 jit_solution(10623460912670256929)
XLA Ops:
  0.0 3.9 %partial.1 = (bf16[64,5760]{1,0:T(8,128)(2,1)S(1)}, bf16[64,3200]{1,0:T(8,128)(2,1)S(1)}, f32[8,1792]{1,0:T(8,128)S(1)}, s32[15]{0:T(128)S(4)}, s32[1]{0:T(128)S(4)}) custom-call(bf16[64,8192]{1,0:T(8,128)(2,1)} %tokens_hbm.1, f32[1,8192]{1,0:T(1,128)} %bitcast.20, bf16[16,8192]{1,0:T(8,128)(2,1)} %hot_gate_hbm.1, bf16[16,8192]{1,0:T(8,128)(2,1)} %hot_up_hbm.1, ...), custom_call_target="tpu_custom_call" | custom-call | tf_op jit(solution)/shard_map/partial/pallas_call | solution.py:279
  3.9 31.1 %conditional.1 = ((f32[64,256]{1,0:T(8,128)S(1)}, bf16[64,256]{1,0:T(8,128)(2,1)S(1)}, bf16[64,256]{1,0:T(8,128)(2,1)S(1)}, bf16[64,256]{1,0:T(8,128)(2,1)S(1)})) conditional(s32[]{:T(128)} %bitcast.11, (bf16[64,5760]{1,0:T(8,128)(2,1)S(1)}, f32[8,1792]{1,0:T(8,128)S(1)}, s32[15]{0:T(128)S(4)}, bf16[3584,1024]{1,0:T(8,128)(2,1)}) %tuple.11, ...), branch_computations={%region_0.0_spmd, %region_1.0_spmd} | conditional | bytes 1966088 | solution.py:347
  4.0 19.4 %all_to_all.34 = bf16[8,8,3200]{2,1,0:T(8,128)(2,1)S(1)} all-to-all(bf16[8,8,3200]{2,1,0:T(8,128)(2,1)S(1)} %bitcast.16), channel_id=1, replica_groups=mesh['hot'=8,'cold'=4] {'hot'}, dimensions={0} | all-to-all | bytes 819200 | tf_op jit(solution)/shard_map/cond/branch_1_fun/all_to_all | solution.py:313
  23.4 10.1 %all_to_all.35 = bf16[8,8,640]{2,1,0:T(8,128)(2,1)S(1)} all-to-all(bf16[8,8,640]{2,1,0:T(8,128)(2,1)S(1)} %bitcast.19), channel_id=1, replica_groups=mesh['hot'=8,'cold'=4] {'hot'}, dimensions={0} | all-to-all | bytes 163840 | tf_op jit(solution)/shard_map/cond/branch_1_fun/all_to_all | solution.py:331
  33.5 1.5 %down.3 = (f32[64,256]{1,0:T(8,128)S(1)}, bf16[64,256]{1,0:T(8,128)(2,1)S(1)}, bf16[64,256]{1,0:T(8,128)(2,1)S(1)}, bf16[64,256]{1,0:T(8,128)(2,1)S(1)}) custom-call(s32[15]{0:T(128)S(4)} %get-tuple-element.27.picks, bf16[64,640]{1,0:T(8,128)(2,1)S(1)} %bitcast.17, bf16[128,1024]{1,0:T(8,128)(2,1)S(1)} %get-tuple-element.31.hot_rows, ...), custom_call_target="tpu_custom_call" | custom-call | tf_op jit(solution)/shard_map/cond/branch_1_fun/down/pallas_call | solution.py:333
  35.0 0.1 collective-permute-start
  35.1 6.9 %collective-permute-start.1 = (bf16[64,256]{1,0:T(8,128)(2,1)S(1)}, bf16[64,256]{1,0:T(8,128)(2,1)S(1)}, u32[]{:S(2)}, u32[]{:S(2)}) collective-permute-start(bf16[64,256]{1,0:T(8,128)(2,1)S(1)} %get-tuple-element.49), channel_id=1, source_target_pairs={{0,2},{1,3},{2,0},{3,1},{4,6},{5,7},{6,4},{7,5},{8,10},{9,11},{10,... | collective-permute-start | bytes 98312 | tf_op jit(solution)/shard_map/ppermute | solution.py:354
  42.0 0.0 collective-permute-start.2
  42.0 0.0 collective-permute-done
  42.0 1.9 %collective-permute-done.1 = bf16[64,256]{1,0:T(8,128)(2,1)S(1)} collective-permute-done((bf16[64,256]{1,0:T(8,128)(2,1)S(1)}, bf16[64,256]{1,0:T(8,128)(2,1)S(1)}, u32[]{:S(2)}, u32[]{:S(2)}) %collective-permute-start.1) | collective-permute-done | bytes 32800 | tf_op jit(solution)/shard_map/ppermute | solution.py:354
  43.9 1.8 %collective-permute-done.2 = bf16[64,256]{1,0:T(8,128)(2,1)S(1)} collective-permute-done((bf16[64,256]{1,0:T(8,128)(2,1)S(1)}, bf16[64,256]{1,0:T(8,128)(2,1)S(1)}, u32[]{:S(2)}, u32[]{:S(2)}) %collective-permute-start.2) | collective-permute-done | bytes 32800 | tf_op jit(solution)/shard_map/ppermute | solution.py:354
  45.7 0.6 %add_convert_fusion = bf16[64,256]{1,0:T(8,128)(2,1)} fusion(bf16[64,256]{1,0:T(8,128)(2,1)S(1)} %collective-permute-done.2, bf16[64,256]{1,0:T(8,128)(2,1)S(1)} %collective-permute-done.1, f32[64,256]{1,0:T(8,128)S(1)} %get-tuple-element.47, bf16[64,256]{1,0:T(8,128)(2,1)S(1)} %collective-permute-done), kind=kLoop, calls=%fused_computation | loop fusion | flops 114688 | bytes 196608 | tf_op jit(solution)/shard_map/convert_element_type | solution.py:356
  (1 shorter events, 0.0 us)
Async XLA Ops:
  35.0 7.0 %collective-permute-start = (bf16[64,256]{1,0:T(8,128)(2,1)S(1)}, bf16[64,256]{1,0:T(8,128)(2,1)S(1)}, u32[]{:S(2)}, u32[]{:S(2)}) collective-permute-start(bf16[64,256]{1,0:T(8,128)(2,1)S(1)} %get-tuple-element.48), channel_id=1, source_target_pairs={{0,1},{1,0},{2,3},{3,2},{4,5},{5,4},{6,7},{7,6},{8,9},{9,8},{10,11... | collective-permute-start | bytes 98312 | tf_op jit(solution)/shard_map/ppermute | solution.py:354
  35.1 8.8 %collective-permute-start.1 = (bf16[64,256]{1,0:T(8,128)(2,1)S(1)}, bf16[64,256]{1,0:T(8,128)(2,1)S(1)}, u32[]{:S(2)}, u32[]{:S(2)}) collective-permute-start(bf16[64,256]{1,0:T(8,128)(2,1)S(1)} %get-tuple-element.49), channel_id=1, source_target_pairs={{0,2},{1,3},{2,0},{3,1},{4,6},{5,7},{6,4},{7,5},{8,10},{9,11},{10,... | collective-permute-start | bytes 98312 | tf_op jit(solution)/shard_map/ppermute | solution.py:354
  42.0 3.7 %collective-permute-start.2 = (bf16[64,256]{1,0:T(8,128)(2,1)S(1)}, bf16[64,256]{1,0:T(8,128)(2,1)S(1)}, u32[]{:S(2)}, u32[]{:S(2)}) collective-permute-start(bf16[64,256]{1,0:T(8,128)(2,1)S(1)} %get-tuple-element.50), channel_id=1, source_target_pairs={{0,3},{1,2},{2,1},{3,0},{4,7},{5,6},{6,5},{7,4},{8,11},{9,10},{10,... | collective-permute-start | bytes 98312 | tf_op jit(solution)/shard_map/ppermute | solution.py:354

commit v4 on v3

--- a/solution.py
+++ b/solution.py
@@ -13,6 +13,7 @@
 VMEM = pl.BlockSpec(memory_space=pltpu.VMEM)
 SMEM = pl.BlockSpec(memory_space=pltpu.SMEM)
 NT = (((1,), (1,)), ((), ()))
+EARLY_ALL, EARLY_FEW = True, False
 
 
 def limit(mib):
@@ -26,9 +27,9 @@
 def partial_kernel(
     tokens_hbm, gain_hbm, hot_gate_hbm, hot_up_hbm, hot_index_hbm, mask_hbm, cold_gate, cold_up,
     hot_down,
-    out, few, live, picks, flag,
+    out, few, late_rows, live, picks, flag,
     tokens, gain, hot_w, hot_index, mask, normed_v, unit_v, w_v, in_sem, w_sem, row_sem,
-    *, slots, block, n_hot, fold,
+    *, slots, few_slots, block, n_hot, early,
 ):
     rows = hot_gate_hbm.shape[0]
     loads = [
@@ -50,7 +51,9 @@
     start = rows * n_hot
     cols = hot_down.shape[1] // n_hot
     chunk = live.shape[0]
-    base = start + (rows // chunk * cols if fold else 0)
+    row_lanes = rows // chunk * cols
+    base = out.shape[1] - 2 * slots * block
+    few_base = few.shape[1] - 2 * few_slots * block
     mask_f = mask[...].astype(F32)
     alive = jnp.max(mask_f, axis=1, keepdims=True)
     tri = (
@@ -62,7 +65,7 @@
     number = lax.broadcasted_iota(jnp.int32, (blocks, 1), 0).astype(F32)
     count = jnp.sum(alive).astype(jnp.int32)
     picks[slots] = count
-    flag[0] = jnp.where(count <= (few.shape[1] - base) // (2 * block), 1, 0)
+    flag[0] = jnp.where(count <= few_slots, 1, 0)
     index = []
     for j in range(slots):
         index.append(jnp.sum(jnp.where(rank == float(j + 1), number, 0.0)).astype(jnp.int32))
@@ -87,13 +90,14 @@
                 copy.start()
 
     row_copies = []
-    if fold:
+    targets = [] if early is None else [(late_rows, 0)] + [(out, start)] * early
+    for which, (target, lane0) in enumerate(targets):
         for dst in range(n_hot):
             for i in range(rows // chunk):
                 row_copies.append(pltpu.make_async_copy(
                     hot_down.at[pl.ds(i * chunk, chunk), pl.ds(dst * cols, cols)],
-                    out.at[pl.ds(dst * chunk, chunk), pl.ds(start + i * cols, cols)],
-                    row_sem.at[dst, i],
+                    target.at[pl.ds(dst * chunk, chunk), pl.ds(lane0 + i * cols, cols)],
+                    row_sem.at[which, dst, i],
                 ))
     for copy in row_copies:
         copy.start()
@@ -136,10 +140,10 @@
     loads[5].wait()
     both = lax.dot_general(normed_v[...], hot_w[...], NT, preferred_element_type=F32)
     hidden_hot = (silu(both[:, :rows]) * both[:, rows:]).astype(BF16)
-    spread = (
-        lax.broadcasted_iota(jnp.int32, (rows, rows * n_hot), 1)
-        == lax.broadcasted_iota(jnp.int32, (rows, rows * n_hot), 0) + h * rows
-    ).astype(BF16)
+    part = chunk if early is not None else rows
+    row = lax.broadcasted_iota(jnp.int32, (rows, rows * n_hot), 0)
+    place = row // part * (n_hot * part) + h * part + row % part
+    spread = (lax.broadcasted_iota(jnp.int32, (rows, rows * n_hot), 1) == place).astype(BF16)
     out[:, pl.ds(0, rows * n_hot)] = jnp.dot(
         hidden_hot, spread, preferred_element_type=F32
     ).astype(BF16)
@@ -161,12 +165,16 @@
     for copy in row_copies:
         copy.wait()
 
-    @pl.when(count <= (few.shape[1] - base) // (2 * block))
+    @pl.when(count <= few_slots)
     def _():
-        few[...] = out[:, pl.ds(0, few.shape[1])]
-
-
-def hidden_kernel(parts, live, out, *hot_rows, slots, block, n_hot, hot_lanes):
+        few[:, pl.ds(0, start)] = out[:, pl.ds(0, start)]
+        if few_base > start:
+            few[:, pl.ds(start, row_lanes)] = late_rows[...]
+        lanes = 2 * few_slots * block
+        few[:, pl.ds(few_base, lanes)] = out[:, pl.ds(base, lanes)]
+
+
+def hidden_kernel(parts, live, late_rows, out, *hot_rows, slots, block, n_hot, hot_lanes):
     chunk = live.shape[0]
     base = parts.shape[1] - 2 * slots * block
 
@@ -185,19 +193,18 @@
         pieces.append((silu(gate) * up * live[:, pl.ds(j * block, block)]).astype(BF16))
     pieces.append(total(0, hot_lanes).astype(BF16))
     hidden = jnp.concatenate(pieces, axis=1)
+    width = hidden.shape[1]
     for dst in range(n_hot):
-        out[pl.ds(dst * chunk, chunk), :] = hidden
+        out[pl.ds(dst * chunk, chunk), pl.ds(0, width)] = hidden
+    if out.shape[1] > width:
+        out[:, pl.ds(width, late_rows.shape[1])] = late_rows[...]
     for rows in hot_rows:
-        cols = rows.shape[1]
-        each = hot_lanes // n_hot // chunk
-        for src in range(n_hot):
-            for i in range(each):
-                rows[pl.ds((src * each + i) * chunk, chunk), :] = parts[
-                    pl.ds(src * chunk, chunk), pl.ds(hot_lanes + i * cols, cols)
-                ]
-
-
-def down_kernel(picks, hidden, hot_rows, cold_down, own, *rest, slots, block):
+        seqs, cols = parts.shape[0], rows.shape[1]
+        for i in range(rows.shape[0] // seqs):
+            rows[pl.ds(i * seqs, seqs), :] = parts[:, pl.ds(hot_lanes + i * cols, cols)]
+
+
+def down_kernel(picks, hidden, hot_rows, cold_down, own, *rest, slots, block, late):
     sends, (total, w, sem) = rest[:-3], rest[-3:]
     count = picks[picks.shape[0] - 1]
     group = 2 if slots % 2 == 0 else 1
@@ -217,9 +224,20 @@
             w[pl.ds(j * block, block), :] = jnp.zeros((block, w.shape[1]), BF16)
 
     base = slots * block
-    total[...] = jnp.dot(
-        hidden[:, pl.ds(base, hot_rows.shape[0])], hot_rows[...], preferred_element_type=F32
-    )
+    if late:
+        seqs, cols = total.shape
+        hot_lanes = hidden.shape[1] - base - late
+        total[...] = jnp.zeros(total.shape, F32)
+        for i in range(hot_lanes // seqs):
+            total[...] += jnp.dot(
+                hidden[:, pl.ds(base + i * seqs, seqs)],
+                hidden[:, pl.ds(base + hot_lanes + i * cols, cols)],
+                preferred_element_type=F32,
+            )
+    else:
+        total[...] = jnp.dot(
+            hidden[:, pl.ds(base, hot_rows.shape[0])], hot_rows[...], preferred_element_type=F32
+        )
     for first in range(0, slots, group):
 
         @pl.when(first < count)
@@ -273,20 +291,22 @@
 
     fold = chunk % 8 == 0 and rows % chunk == 0
     row_lanes = rows // chunk * cols if fold else 0
-    shared = hot_lanes + row_lanes
     few = max(2, slots // 6 * 2)
-
-    parts, few_parts, live, picks, flag = pl.pallas_call(
+    early_all, early_few = (EARLY_ALL, EARLY_FEW) if fold else (False, False)
+
+    parts, few_parts, late_rows, live, picks, flag = pl.pallas_call(
         functools.partial(
-            partial_kernel, slots=slots, block=block, n_hot=n_hot, fold=fold
+            partial_kernel, slots=slots, few_slots=few, block=block, n_hot=n_hot,
+            early=early_all if fold else None,
         ),
         name="partial",
         compiler_params=limit(20),
         in_specs=[ANY] * 9,
-        out_specs=[VMEM, VMEM, VMEM, SMEM, SMEM],
+        out_specs=[VMEM] * 4 + [SMEM] * 2,
         out_shape=[
-            pltpu.VMEM((seqs, shared + 2 * slots * block), BF16),
-            pltpu.VMEM((seqs, shared + 2 * few * block), BF16),
+            pltpu.VMEM((seqs, hot_lanes + early_all * row_lanes + 2 * slots * block), BF16),
+            pltpu.VMEM((seqs, hot_lanes + early_few * row_lanes + 2 * few * block), BF16),
+            pltpu.VMEM((seqs, max(128, row_lanes)), BF16),
             pltpu.VMEM((chunk, slots * block), F32),
             pltpu.SMEM((slots + 1,), jnp.int32),
             pltpu.SMEM((1,), jnp.int32),
@@ -302,14 +322,15 @@
             pltpu.VMEM((slots, feats, 2 * block), BF16),
             pltpu.SemaphoreType.DMA((6,)),
             pltpu.SemaphoreType.DMA((2, slots)),
-            pltpu.SemaphoreType.DMA((n_hot, max(1, rows // chunk))),
+            pltpu.SemaphoreType.DMA((2, n_hot, max(1, rows // chunk))),
         ],
     )(*(in_hbm(value) for value in (
         tokens, norm_gain[None, :], hot_gate, hot_up, hot_index[None, :],
         block_mask.T, cold_gate, cold_up, hot_down,
     )))
 
-    def middle(slots, parts, live, picks, hot_down, cold_down):
+    def middle(slots, early, parts, late_rows, live, picks, hot_down, cold_down):
+        late = 0 if early else row_lanes
         parts = lax.all_to_all(parts, "hot", split_axis=0, concat_axis=0, tiled=True)
         hidden, *moved = pl.pallas_call(
             functools.partial(
@@ -317,21 +338,23 @@
             ),
             name="hidden",
             compiler_params=limit(8),
-            in_specs=[VMEM, VMEM],
-            out_specs=[VMEM] * (1 + fold),
+            in_specs=[VMEM] * 3,
+            out_specs=[VMEM] * (1 + early),
             out_shape=[
-                pltpu.VMEM((seqs, slots * block + hot_lanes), BF16),
+                pltpu.VMEM((seqs, slots * block + hot_lanes + late), BF16),
                 pltpu.VMEM((hot_lanes, cols), BF16),
-            ][: 1 + fold],
-        )(in_vmem(parts), in_vmem(live))
-        if fold:
+            ][: 1 + early],
+        )(in_vmem(parts), in_vmem(live), in_vmem(late_rows))
+        if early:
             hot_rows = moved[0]
+        elif late:
+            hot_rows = late_rows
         else:
             hot_rows = lax.all_to_all(hot_down, "hot", split_axis=1, concat_axis=0, tiled=True)
         hidden = lax.all_to_all(hidden, "hot", split_axis=0, concat_axis=0, tiled=True)
         piece = (seqs, cols // n_cold)
         return tuple(pl.pallas_call(
-            functools.partial(down_kernel, slots=slots, block=block),
+            functools.partial(down_kernel, slots=slots, block=block, late=late),
             name="down",
             compiler_params=limit(8),
             in_specs=[SMEM, VMEM, VMEM, ANY],
@@ -346,9 +369,9 @@
 
     own, *sends = lax.cond(
         flag[0] > 0,
-        lambda parts, few_parts, *rest: middle(few, few_parts, *rest),
-        lambda parts, few_parts, *rest: middle(slots, parts, *rest),
-        parts, few_parts, live, picks, hot_down, cold_down,
+        lambda parts, few_parts, *rest: middle(few, early_few, few_parts, *rest),
+        lambda parts, few_parts, *rest: middle(slots, early_all, parts, *rest),
+        parts, few_parts, late_rows, live, picks, hot_down, cold_down,
     )
     for k, send in enumerate(sends):
         got = lax.ppermute(send, "cold", [(i, i ^ (k + 1)) for i in range(n_cold)])

time: 46.6 us -> 44 us (0.944)
  blocking collectives: 29.5 us -> 27.1 us
    all_to_all x1, blocking collectives: 19.4 us -> 14.6 us  [middle(): lax.all_to_all(parts, 'hot', split_axis=0, concat_axis=0, tiled=True)]
    all_to_all x1, blocking collectives: 10.1 us -> 12.5 us  [middle(): lax.all_to_all(hidden, 'hot', split_axis=0, concat_axis=0, tiled=True)]
where the time goes in v4:
time: 44 us; the launch traced here: 43.7 us
  blocking collectives  27.1 us (62%)
  starting transfers between devices  6.61 us (15%)
  Pallas kernels  5.62 us (13%)
  waiting for transfers between devices  3.66 us (8%)
  other arithmetic  0.63 us (1%)
    all_to_all x1, blocking collectives, middle(): lax.all_to_all(parts, 'hot', split_axis=0, concat_axis=0, tiled=True)  14.6 us
    all_to_all x1, blocking collectives, middle(): lax.all_to_all(hidden, 'hot', split_axis=0, concat_axis=0, tiled=True)  12.5 us
    ppermute x3, starting transfers between devices, on_device(): got = lax.ppermute(send, 'cold', [(i, i ^ k + 1) for i in range(n_cold)])  6.61 us
    pallas_call x1, Pallas kernels, on_device(): pl.pallas_call(functools.partial(partial_kernel, slots=slots, few_slots=f...  4.07 us
    ppermute x3, waiting for transfers between devices, on_device(): got = lax.ppermute(send, 'cold', [(i, i ^ k + 1) for i in range(n_cold)])  3.66 us
    pallas_call x1, Pallas kernels, middle(): pl.pallas_call(functools.partial(down_kernel, slots=slots, block=block, l...  1.51 us
  transfers between devices with their start and end apart: 3, of which 2 were waited for; matrix products, arithmetic and copies ran while one was open for 0% of the time, Pallas kernels for 0%

profile of v4, /device:TPU:0, one launch (start us, length us, event | category | flops | bytes accessed | tf_op | source)
XLA Modules:
  0.0 43.7 jit_solution(11019847843668725840)
XLA Ops:
  0.0 4.1 %partial.1 = (bf16[64,5760]{1,0:T(8,128)(2,1)S(1)}, bf16[64,1152]{1,0:T(8,128)(2,1)S(1)}, bf16[64,2048]{1,0:T(8,128)(2,1)S(1)}, f32[8,1792]{1,0:T(8,128)S(1)}, s32[15]{0:T(128)S(4)}, /*index=5*/s32[1]{0:T(128)S(4)}) custom-call(bf16[64,8192]{1,0:T(8,128)(2,1)} %tokens_hbm.1, f32[1,8192]{1,0:T(1,128)} %bitcast.20, bf16[16,8192]{1,0:T(8,128)(2,1)} %hot_gate_hbm.1, ...), custom_call_target="tpu_custom_call" | custom-call | tf_op jit(solution)/shard_map/partial/pallas_call | solution.py:297
  4.1 28.7 %conditional.1 = ((f32[64,256]{1,0:T(8,128)S(1)}, bf16[64,256]{1,0:T(8,128)(2,1)S(1)}, bf16[64,256]{1,0:T(8,128)(2,1)S(1)}, bf16[64,256]{1,0:T(8,128)(2,1)S(1)})) conditional(s32[]{:T(128)} %bitcast.11, (bf16[64,5760]{1,0:T(8,128)(2,1)S(1)}, f32[8,1792]{1,0:T(8,128)S(1)}, bf16[64,2048]{1,0:T(8,128)(2,1)S(1)}, s32[15]{0:T(128)S(4)}, ...), branch_computations={%region_0.0_spmd, %region_1.0_spmd} | conditional | bytes 1966088 | solution.py:370
  4.1 14.6 %all_to_all.34 = bf16[8,8,1152]{2,1,0:T(8,128)(2,1)S(1)} all-to-all(bf16[8,8,1152]{2,1,0:T(8,128)(2,1)S(1)} %bitcast.19), channel_id=1, replica_groups=mesh['hot'=8,'cold'=4] {'hot'}, dimensions={0} | all-to-all | bytes 294912 | tf_op jit(solution)/shard_map/cond/branch_1_fun/all_to_all | solution.py:334
  18.7 12.5 %all_to_all.35 = bf16[8,8,2688]{2,1,0:T(8,128)(2,1)S(1)} all-to-all(bf16[8,8,2688]{2,1,0:T(8,128)(2,1)S(1)} %bitcast.14), channel_id=1, replica_groups=mesh['hot'=8,'cold'=4] {'hot'}, dimensions={0} | all-to-all | bytes 688128 | tf_op jit(solution)/shard_map/cond/branch_1_fun/all_to_all | solution.py:354
  31.2 1.5 %down.3 = (f32[64,256]{1,0:T(8,128)S(1)}, bf16[64,256]{1,0:T(8,128)(2,1)S(1)}, bf16[64,256]{1,0:T(8,128)(2,1)S(1)}, bf16[64,256]{1,0:T(8,128)(2,1)S(1)}) custom-call(s32[15]{0:T(128)S(4)} %get-tuple-element.32.picks, bf16[64,2688]{1,0:T(8,128)(2,1)S(1)} %bitcast.13, bf16[64,2048]{1,0:T(8,128)(2,1)S(1)} %get-tuple-element.35.late_rows.hot_rows, ...), custom_call_target="tpu_custom_call" | custom-call | tf_op jit(solution)/shard_map/cond/branch_1_fun/down/pallas_call | solution.py:356
  32.7 0.1 collective-permute-start
  32.8 6.5 %collective-permute-start.1 = (bf16[64,256]{1,0:T(8,128)(2,1)S(1)}, bf16[64,256]{1,0:T(8,128)(2,1)S(1)}, u32[]{:S(2)}, u32[]{:S(2)}) collective-permute-start(bf16[64,256]{1,0:T(8,128)(2,1)S(1)} %get-tuple-element.55), channel_id=1, source_target_pairs={{0,2},{1,3},{2,0},{3,1},{4,6},{5,7},{6,4},{7,5},{8,10},{9,11},{10,... | collective-permute-start | bytes 98312 | tf_op jit(solution)/shard_map/ppermute | solution.py:377
  39.4 0.0 collective-permute-start.2
  39.4 0.0 collective-permute-done
  39.4 1.9 %collective-permute-done.1 = bf16[64,256]{1,0:T(8,128)(2,1)S(1)} collective-permute-done((bf16[64,256]{1,0:T(8,128)(2,1)S(1)}, bf16[64,256]{1,0:T(8,128)(2,1)S(1)}, u32[]{:S(2)}, u32[]{:S(2)}) %collective-permute-start.1) | collective-permute-done | bytes 32800 | tf_op jit(solution)/shard_map/ppermute | solution.py:377
  41.2 1.8 %collective-permute-done.2 = bf16[64,256]{1,0:T(8,128)(2,1)S(1)} collective-permute-done((bf16[64,256]{1,0:T(8,128)(2,1)S(1)}, bf16[64,256]{1,0:T(8,128)(2,1)S(1)}, u32[]{:S(2)}, u32[]{:S(2)}) %collective-permute-start.2) | collective-permute-done | bytes 32800 | tf_op jit(solution)/shard_map/ppermute | solution.py:377
  43.0 0.6 %add_convert_fusion = bf16[64,256]{1,0:T(8,128)(2,1)} fusion(bf16[64,256]{1,0:T(8,128)(2,1)S(1)} %collective-permute-done.2, bf16[64,256]{1,0:T(8,128)(2,1)S(1)} %collective-permute-done.1, f32[64,256]{1,0:T(8,128)S(1)} %get-tuple-element.53, bf16[64,256]{1,0:T(8,128)(2,1)S(1)} %collective-permute-done), kind=kLoop, calls=%fused_computation | loop fusion | flops 114688 | bytes 196608 | tf_op jit(solution)/shard_map/convert_element_type | solution.py:379
  (1 shorter events, 0.0 us)
Async XLA Ops:
  32.7 6.6 %collective-permute-start = (bf16[64,256]{1,0:T(8,128)(2,1)S(1)}, bf16[64,256]{1,0:T(8,128)(2,1)S(1)}, u32[]{:S(2)}, u32[]{:S(2)}) collective-permute-start(bf16[64,256]{1,0:T(8,128)(2,1)S(1)} %get-tuple-element.54), channel_id=1, source_target_pairs={{0,1},{1,0},{2,3},{3,2},{4,5},{5,4},{6,7},{7,6},{8,9},{9,8},{10,11... | collective-permute-start | bytes 98312 | tf_op jit(solution)/shard_map/ppermute | solution.py:377
  32.8 8.4 %collective-permute-start.1 = (bf16[64,256]{1,0:T(8,128)(2,1)S(1)}, bf16[64,256]{1,0:T(8,128)(2,1)S(1)}, u32[]{:S(2)}, u32[]{:S(2)}) collective-permute-start(bf16[64,256]{1,0:T(8,128)(2,1)S(1)} %get-tuple-element.55), channel_id=1, source_target_pairs={{0,2},{1,3},{2,0},{3,1},{4,6},{5,7},{6,4},{7,5},{8,10},{9,11},{10,... | collective-permute-start | bytes 98312 | tf_op jit(solution)/shard_map/ppermute | solution.py:377
  39.4 3.7 %collective-permute-start.2 = (bf16[64,256]{1,0:T(8,128)(2,1)S(1)}, bf16[64,256]{1,0:T(8,128)(2,1)S(1)}, u32[]{:S(2)}, u32[]{:S(2)}) collective-permute-start(bf16[64,256]{1,0:T(8,128)(2,1)S(1)} %get-tuple-element.56), channel_id=1, source_target_pairs={{0,3},{1,2},{2,1},{3,0},{4,7},{5,6},{6,5},{7,4},{8,11},{9,10},{10,... | collective-permute-start | bytes 98312 | tf_op jit(solution)/shard_map/ppermute | solution.py:377

commit v5 on v4

--- a/solution.py
+++ b/solution.py
@@ -13,7 +13,6 @@
 VMEM = pl.BlockSpec(memory_space=pltpu.VMEM)
 SMEM = pl.BlockSpec(memory_space=pltpu.SMEM)
 NT = (((1,), (1,)), ((), ()))
-EARLY_ALL, EARLY_FEW = True, False
 
 
 def limit(mib):
@@ -27,9 +26,9 @@
 def partial_kernel(
     tokens_hbm, gain_hbm, hot_gate_hbm, hot_up_hbm, hot_index_hbm, mask_hbm, cold_gate, cold_up,
     hot_down,
-    out, few, late_rows, live, picks, flag,
+    wide, out, few_wide, few, row_out, live, picks, branch,
     tokens, gain, hot_w, hot_index, mask, normed_v, unit_v, w_v, in_sem, w_sem, row_sem,
-    *, slots, few_slots, block, n_hot, early,
+    *, slots, few_slots, block, n_hot, fold,
 ):
     rows = hot_gate_hbm.shape[0]
     loads = [
@@ -51,9 +50,7 @@
     start = rows * n_hot
     cols = hot_down.shape[1] // n_hot
     chunk = live.shape[0]
-    row_lanes = rows // chunk * cols
-    base = out.shape[1] - 2 * slots * block
-    few_base = few.shape[1] - 2 * few_slots * block
+    base = start
     mask_f = mask[...].astype(F32)
     alive = jnp.max(mask_f, axis=1, keepdims=True)
     tri = (
@@ -65,7 +62,7 @@
     number = lax.broadcasted_iota(jnp.int32, (blocks, 1), 0).astype(F32)
     count = jnp.sum(alive).astype(jnp.int32)
     picks[slots] = count
-    flag[0] = jnp.where(count <= few_slots, 1, 0)
+    branch[0] = jnp.where(count <= few_slots, 0, 1) + 2 * (c % 2)
     index = []
     for j in range(slots):
         index.append(jnp.sum(jnp.where(rank == float(j + 1), number, 0.0)).astype(jnp.int32))
@@ -90,14 +87,13 @@
                 copy.start()
 
     row_copies = []
-    targets = [] if early is None else [(late_rows, 0)] + [(out, start)] * early
-    for which, (target, lane0) in enumerate(targets):
+    if fold:
         for dst in range(n_hot):
             for i in range(rows // chunk):
                 row_copies.append(pltpu.make_async_copy(
                     hot_down.at[pl.ds(i * chunk, chunk), pl.ds(dst * cols, cols)],
-                    target.at[pl.ds(dst * chunk, chunk), pl.ds(lane0 + i * cols, cols)],
-                    row_sem.at[which, dst, i],
+                    row_out.at[pl.ds(dst * chunk, chunk), pl.ds(i * cols, cols)],
+                    row_sem.at[dst, i],
                 ))
     for copy in row_copies:
         copy.start()
@@ -140,7 +136,7 @@
     loads[5].wait()
     both = lax.dot_general(normed_v[...], hot_w[...], NT, preferred_element_type=F32)
     hidden_hot = (silu(both[:, :rows]) * both[:, rows:]).astype(BF16)
-    part = chunk if early is not None else rows
+    part = chunk if fold else rows
     row = lax.broadcasted_iota(jnp.int32, (rows, rows * n_hot), 0)
     place = row // part * (n_hot * part) + h * part + row % part
     spread = (lax.broadcasted_iota(jnp.int32, (rows, rows * n_hot), 1) == place).astype(BF16)
@@ -165,13 +161,24 @@
     for copy in row_copies:
         copy.wait()
 
-    @pl.when(count <= few_slots)
+    def fill(target, lanes):
+        target[:, pl.ds(0, start)] = out[:, pl.ds(0, start)]
+        shift = target.shape[1] - start - lanes
+        if shift:
+            target[:, pl.ds(start, shift)] = row_out[...]
+        target[:, pl.ds(start + shift, lanes)] = out[:, pl.ds(start, lanes)]
+
+    @pl.when(branch[0] == 0)
     def _():
-        few[:, pl.ds(0, start)] = out[:, pl.ds(0, start)]
-        if few_base > start:
-            few[:, pl.ds(start, row_lanes)] = late_rows[...]
-        lanes = 2 * few_slots * block
-        few[:, pl.ds(few_base, lanes)] = out[:, pl.ds(base, lanes)]
+        fill(few, 2 * few_slots * block)
+
+    @pl.when(branch[0] == 2)
+    def _():
+        fill(few_wide, 2 * few_slots * block)
+
+    @pl.when(branch[0] == 3)
+    def _():
+        fill(wide, 2 * slots * block)
 
 
 def hidden_kernel(parts, live, late_rows, out, *hot_rows, slots, block, n_hot, hot_lanes):
@@ -292,20 +299,21 @@
     fold = chunk % 8 == 0 and rows % chunk == 0
     row_lanes = rows // chunk * cols if fold else 0
     few = max(2, slots // 6 * 2)
-    early_all, early_few = (EARLY_ALL, EARLY_FEW) if fold else (False, False)
-
-    parts, few_parts, late_rows, live, picks, flag = pl.pallas_call(
+
+    *sent, late_rows, live, picks, branch = pl.pallas_call(
         functools.partial(
             partial_kernel, slots=slots, few_slots=few, block=block, n_hot=n_hot,
-            early=early_all if fold else None,
+            fold=fold,
         ),
         name="partial",
         compiler_params=limit(20),
         in_specs=[ANY] * 9,
-        out_specs=[VMEM] * 4 + [SMEM] * 2,
+        out_specs=[VMEM] * 6 + [SMEM] * 2,
         out_shape=[
-            pltpu.VMEM((seqs, hot_lanes + early_all * row_lanes + 2 * slots * block), BF16),
-            pltpu.VMEM((seqs, hot_lanes + early_few * row_lanes + 2 * few * block), BF16),
+            pltpu.VMEM((seqs, hot_lanes + row_lanes + 2 * slots * block), BF16),
+            pltpu.VMEM((seqs, hot_lanes + 2 * slots * block), BF16),
+            pltpu.VMEM((seqs, hot_lanes + row_lanes + 2 * few * block), BF16),
+            pltpu.VMEM((seqs, hot_lanes + 2 * few * block), BF16),
             pltpu.VMEM((seqs, max(128, row_lanes)), BF16),
             pltpu.VMEM((chunk, slots * block), F32),
             pltpu.SMEM((slots + 1,), jnp.int32),
@@ -322,7 +330,7 @@
             pltpu.VMEM((slots, feats, 2 * block), BF16),
             pltpu.SemaphoreType.DMA((6,)),
             pltpu.SemaphoreType.DMA((2, slots)),
-            pltpu.SemaphoreType.DMA((2, n_hot, max(1, rows // chunk))),
+            pltpu.SemaphoreType.DMA((n_hot, max(1, rows // chunk))),
         ],
     )(*(in_hbm(value) for value in (
         tokens, norm_gain[None, :], hot_gate, hot_up, hot_index[None, :],
@@ -367,13 +375,19 @@
             ],
         )(pltpu.with_memory_space_constraint(picks, pltpu.SMEM), in_vmem(hidden), in_vmem(hot_rows), in_hbm(cold_down)))
 
-    own, *sends = lax.cond(
-        flag[0] > 0,
-        lambda parts, few_parts, *rest: middle(few, early_few, few_parts, *rest),
-        lambda parts, few_parts, *rest: middle(slots, early_all, parts, *rest),
-        parts, few_parts, late_rows, live, picks, hot_down, cold_down,
+    wide, narrow, few_wide, few_narrow = sent
+    own, *sends = lax.switch(
+        branch[0],
+        [
+            lambda wide, narrow, few_wide, few_narrow, *rest: middle(few, False, few_narrow, *rest),
+            lambda wide, narrow, few_wide, few_narrow, *rest: middle(slots, False, narrow, *rest),
+            lambda wide, narrow, few_wide, few_narrow, *rest: middle(few, fold, few_wide, *rest),
+            lambda wide, narrow, few_wide, few_narrow, *rest: middle(slots, fold, wide, *rest),
+        ],
+        wide, narrow, few_wide, few_narrow, late_rows, live, picks, hot_down, cold_down,
     )
-    for k, send in enumerate(sends):
+    for k in [*range(1, n_cold - 1), 0]:
+        send = sends[k]
         got = lax.ppermute(send, "cold", [(i, i ^ (k + 1)) for i in range(n_cold)])
         own = own + got.astype(F32)
     return own.astype(BF16)

time: 44 us -> 42.7 us (0.970)
  the two profiles are of different devices: /device:TPU:0 before, /device:TPU:1 now
where the time goes in v5:
time: 42.7 us; the launch traced here: 42.4 us
  blocking collectives  24.8 us (58%)
  starting transfers between devices  8.63 us (20%)
  Pallas kernels  5.42 us (13%)
  waiting for transfers between devices  2.87 us (7%)
  other arithmetic  0.64 us (1%)
    all_to_all x1, blocking collectives, middle(): lax.all_to_all(parts, 'hot', split_axis=0, concat_axis=0, tiled=True)  15.9 us
    all_to_all x1, blocking collectives, middle(): lax.all_to_all(hidden, 'hot', split_axis=0, concat_axis=0, tiled=True)  8.86 us
    ppermute x3, starting transfers between devices, on_device(): got = lax.ppermute(send, 'cold', [(i, i ^ k + 1) for i in range(n_cold)])  8.63 us
    pallas_call x1, Pallas kernels, on_device(): pl.pallas_call(functools.partial(partial_kernel, slots=slots, few_slots=f...  3.88 us
    ppermute x3, waiting for transfers between devices, on_device(): got = lax.ppermute(send, 'cold', [(i, i ^ k + 1) for i in range(n_cold)])  2.87 us
    pallas_call x1, Pallas kernels, middle(): pl.pallas_call(functools.partial(down_kernel, slots=slots, block=block, l...  1.51 us
  transfers between devices with their start and end apart: 3, of which 2 were waited for; matrix products, arithmetic and copies ran while one was open for 0% of the time, Pallas kernels for 0%

profile of v5, /device:TPU:1, one launch (start us, length us, event | category | flops | bytes accessed | tf_op | source)
XLA Modules:
  0.0 42.4 jit_solution(4851755395063918589)
XLA Ops:
  0.0 3.9 %partial.1 = (bf16[64,5760]{1,0:T(8,128)(2,1)S(1)}, bf16[64,3712]{1,0:T(8,128)(2,1)S(1)}, bf16[64,3200]{1,0:T(8,128)(2,1)S(1)}, bf16[64,1152]{1,0:T(8,128)(2,1)S...) custom-call(bf16[64,8192]{1,0:T(8,128)(2,1)} %tokens_hbm.1, ...), custom_call_target="tpu_custom_call" | custom-call | tf_op jit(solution)/shard_map/partial/pallas_call | solution.py:303
  3.9 26.4 %conditional.1 = ((f32[64,256]{1,0:T(8,128)S(1)}, bf16[64,256]{1,0:T(8,128)(2,1)S(1)}, bf16[64,256]{1,0:T(8,128)(2,1)S(1)}, bf16[64,256]{1,0:T(8,128)(2,1)S(1)})) conditional(s32[]{:T(128)} %bitcast.19, (bf16[64,1152]{1,0:T(8,128)(2,1)S(1)}, f32[8,1792]{1,0:T(8,128)S(1)}, bf16[64,2048]{1,0:T(8,128)(2,1)S(1)}, ...), branch_computations={%region_0.0_spmd, %region_1.0_spmd, %region_2.0_spmd, %region_3.0_... | conditional | bytes 1966088 | solution.py:379
  3.9 15.9 %all_to_all.68 = bf16[8,8,3200]{2,1,0:T(8,128)(2,1)S(1)} all-to-all(bf16[8,8,3200]{2,1,0:T(8,128)(2,1)S(1)} %bitcast.31), channel_id=1, replica_groups=mesh['hot'=8,'cold'=4] {'hot'}, dimensions={0} | all-to-all | bytes 819200 | tf_op jit(solution)/shard_map/cond/branch_2_fun/all_to_all | solution.py:342
  19.9 8.9 %all_to_all.69 = bf16[8,8,640]{2,1,0:T(8,128)(2,1)S(1)} all-to-all(bf16[8,8,640]{2,1,0:T(8,128)(2,1)S(1)} %bitcast.35), channel_id=1, replica_groups=mesh['hot'=8,'cold'=4] {'hot'}, dimensions={0} | all-to-all | bytes 163840 | tf_op jit(solution)/shard_map/cond/branch_2_fun/all_to_all | solution.py:362
  28.8 1.5 %down.6 = (f32[64,256]{1,0:T(8,128)S(1)}, bf16[64,256]{1,0:T(8,128)(2,1)S(1)}, bf16[64,256]{1,0:T(8,128)(2,1)S(1)}, bf16[64,256]{1,0:T(8,128)(2,1)S(1)}) custom-call(s32[15]{0:T(128)S(4)} %get-tuple-element.55.picks, bf16[64,640]{1,0:T(8,128)(2,1)S(1)} %bitcast.32, bf16[128,1024]{1,0:T(8,128)(2,1)S(1)} %get-tuple-element.60.hot_rows, ...), custom_call_target="tpu_custom_call" | custom-call | tf_op jit(solution)/shard_map/cond/branch_2_fun/down/pallas_call | solution.py:364
  30.3 8.2 %collective-permute-start = (bf16[64,256]{1,0:T(8,128)(2,1)S(1)}, bf16[64,256]{1,0:T(8,128)(2,1)S(1)}, u32[]{:S(2)}, u32[]{:S(2)}) collective-permute-start(bf16[64,256]{1,0:T(8,128)(2,1)S(1)} %get-tuple-element.90), channel_id=1, source_target_pairs={{0,2},{1,3},{2,0},{3,1},{4,6},{5,7},{6,4},{7,5},{8,10},{9,11},{10,... | collective-permute-start | bytes 98312 | tf_op jit(solution)/shard_map/ppermute | solution.py:391
  38.4 0.0 collective-permute-start.1
  38.4 0.5 %collective-permute-start.2 = (bf16[64,256]{1,0:T(8,128)(2,1)S(1)}, bf16[64,256]{1,0:T(8,128)(2,1)S(1)}, u32[]{:S(2)}, u32[]{:S(2)}) collective-permute-start(bf16[64,256]{1,0:T(8,128)(2,1)S(1)} %get-tuple-element.92), channel_id=1, source_target_pairs={{0,1},{1,0},{2,3},{3,2},{4,5},{5,4},{6,7},{7,6},{8,9},{9,8},{10,11... | collective-permute-start | bytes 98312 | tf_op jit(solution)/shard_map/ppermute | solution.py:391
  38.9 0.8 %collective-permute-done = bf16[64,256]{1,0:T(8,128)(2,1)S(1)} collective-permute-done((bf16[64,256]{1,0:T(8,128)(2,1)S(1)}, bf16[64,256]{1,0:T(8,128)(2,1)S(1)}, u32[]{:S(2)}, u32[]{:S(2)}) %collective-permute-start) | collective-permute-done | bytes 32800 | tf_op jit(solution)/shard_map/ppermute | solution.py:391
  39.7 2.0 %collective-permute-done.1 = bf16[64,256]{1,0:T(8,128)(2,1)S(1)} collective-permute-done((bf16[64,256]{1,0:T(8,128)(2,1)S(1)}, bf16[64,256]{1,0:T(8,128)(2,1)S(1)}, u32[]{:S(2)}, u32[]{:S(2)}) %collective-permute-start.1) | collective-permute-done | bytes 32800 | tf_op jit(solution)/shard_map/ppermute | solution.py:391
  41.8 0.0 collective-permute-done.2
  41.8 0.6 %add_convert_fusion = bf16[64,256]{1,0:T(8,128)(2,1)} fusion(bf16[64,256]{1,0:T(8,128)(2,1)S(1)} %collective-permute-done.2, bf16[64,256]{1,0:T(8,128)(2,1)S(1)} %collective-permute-done.1, f32[64,256]{1,0:T(8,128)S(1)} %get-tuple-element.89, bf16[64,256]{1,0:T(8,128)(2,1)S(1)} %collective-permute-done), kind=kLoop, calls=%fused_computation | loop fusion | flops 114688 | bytes 196608 | tf_op jit(solution)/shard_map/convert_element_type | solution.py:393
  (1 shorter events, 0.0 us)
Async XLA Ops:
  30.3 9.5 %collective-permute-start = (bf16[64,256]{1,0:T(8,128)(2,1)S(1)}, bf16[64,256]{1,0:T(8,128)(2,1)S(1)}, u32[]{:S(2)}, u32[]{:S(2)}) collective-permute-start(bf16[64,256]{1,0:T(8,128)(2,1)S(1)} %get-tuple-element.90), channel_id=1, source_target_pairs={{0,2},{1,3},{2,0},{3,1},{4,6},{5,7},{6,4},{7,5},{8,10},{9,11},{10,... | collective-permute-start | bytes 98312 | tf_op jit(solution)/shard_map/ppermute | solution.py:391
  38.4 3.3 %collective-permute-start.1 = (bf16[64,256]{1,0:T(8,128)(2,1)S(1)}, bf16[64,256]{1,0:T(8,128)(2,1)S(1)}, u32[]{:S(2)}, u32[]{:S(2)}) collective-permute-start(bf16[64,256]{1,0:T(8,128)(2,1)S(1)} %get-tuple-element.91), channel_id=1, source_target_pairs={{0,3},{1,2},{2,1},{3,0},{4,7},{5,6},{6,5},{7,4},{8,11},{9,10},{10,... | collective-permute-start | bytes 98312 | tf_op jit(solution)/shard_map/ppermute | solution.py:391
  38.4 3.3 %collective-permute-start.2 = (bf16[64,256]{1,0:T(8,128)(2,1)S(1)}, bf16[64,256]{1,0:T(8,128)(2,1)S(1)}, u32[]{:S(2)}, u32[]{:S(2)}) collective-permute-start(bf16[64,256]{1,0:T(8,128)(2,1)S(1)} %get-tuple-element.92), channel_id=1, source_target_pairs={{0,1},{1,0},{2,3},{3,2},{4,5},{5,4},{6,7},{7,6},{8,9},{9,8},{10,11... | collective-permute-start | bytes 98312 | tf_op jit(solution)/shard_map/ppermute | solution.py:391
